TPU v7x, 256 devices: a whole 4x4x8 slice. The times are simulated.
256 devices in a mesh: pipe: 2 (over core), dp: 64 (over z, y, x_lo), tensor: 2 (over x_hi).
Axes of the slice: x: 4 (x_hi: 2, x_lo: 2; x = x_hi * 2 + x_lo), y: 4, z: 8, core: 2. Of those that a mesh axis runs over, the one named last changes fastest.
Arguments:
- hidden_in: bfloat16 [2, 128, 2, 64, 3584], P('pipe', 'dp'), may hold values from -60 to 60, as said below
- attention_probs: bfloat16 [2, 128, 2, 14, 64, 64], P('pipe', 'dp', None, 'tensor'), may hold values from 0 to 1, as said below
- norm_gain: float32 [2, 3584], P('pipe'), may hold values from 0.5 to 1.5
- value_weight: bfloat16 [2, 3584, 256], P('pipe', None, 'tensor'), may hold values from -0.09375 to 0.09375
- output_weight: bfloat16 [2, 1792, 3584], P('pipe', 'tensor'), may hold values from -0.125 to 0.125
- head_grad: bfloat16 [128, 2, 64, 3584], P('dp', 'tensor'), may hold values from -16 to 16
- policy_logprob: float32 [128, 2, 64], P('dp'), may hold values from -3 to -0.2
- reference_logprob: float32 [128, 2], P('dp'), may hold values from -96 to -12.8
- sequence_bounds: int32 [128, 3], P('dp'), may hold values from 1 to 64, as said below
Outputs:
- section_cotangent: bfloat16 [2, 128, 2, 64, 3584], P('pipe', 'dp', 'tensor')
- value_gradient: float32 [2, 3584, 256], P('pipe', 'dp', 'tensor')
- output_gradient: float32 [2, 3584, 1792], P('pipe', 'dp', 'tensor')
- gain_gradient: float32 [2, 3584], P('pipe', 'dp')
Inputs may be any that keep to these rules, and one draw needn't show every extreme that they name: `sequence_bounds`: entry 0 is the prompt length, shared by the two sequences of a pair; a sequence's response is the positions from entry 0 up to its end (entry 1 for the chosen, entry 2 for the rejected sequence), and holds one position or more. `attention_probs`: each row is a causal attention distribution: zero above the diagonal, summing to one before rounding. `hidden_in`: activations of varying size from token to token.
All inputs are finite; a program needn't handle non-finite values.
Results may differ from a plain program's by a relative error of at most 0.017.
Values may be sent and summed in bfloat16 or wider, within the bound.
A program may use at most 128 MiB of HBM per device.

v0:
```python
import jax
import jax.numpy as jnp
from jax import lax
from jax.sharding import PartitionSpec as P

HEAD_DIM = 128


EPSILON = 1e-06
DPO_BETA = 0.25
LIKELIHOOD_COEF = 0.2


def shifted(block, axis, distance):
    devices = range(lax.axis_size(axis))
    route = [(i - distance, i) for i in devices if i - distance in devices]
    return lax.ppermute(block, axis, route)


def copy_for_each(shard, axis):
    copies = jnp.broadcast_to(shard, (lax.axis_size(axis), *shard.shape))
    return lax.all_to_all(copies, axis, split_axis=0, concat_axis=0, tiled=True)


def over_copies(shard, axis):
    everything = copy_for_each(shard, axis)
    return jnp.sum(everything.astype(jnp.float32), axis=0)


def split_up(shard, dim, length):
    before, after = (shard.shape[:dim], shard.shape[dim + 1 :])
    return jnp.moveaxis(shard.reshape(*before, length, -1, *after), dim, 0)


def sent_and_summed(shard, axis, dim):
    length = lax.axis_size(axis)
    parts = lax.all_to_all(split_up(shard, dim, length), axis, 0, 0, tiled=True)
    return jnp.sum(parts, axis=0)


def body(
    hidden_in,
    attention_probs,
    norm_gain,
    value_weight,
    output_weight,
    head_grad,
    policy_logprob,
    reference_logprob,
    sequence_bounds,
):
    section_count = lax.axis_size("pipe")
    section_index = lax.axis_index("pipe")
    tensor_index = lax.axis_index("tensor")
    micro_count = hidden_in.shape[1]
    sequence_length = hidden_in.shape[3]
    model_width = hidden_in.shape[4]
    value_columns = value_weight.shape[2]
    value_heads = value_columns // HEAD_DIM
    local_heads = attention_probs.shape[3]
    group_size = local_heads // value_heads
    mixed_columns = output_weight.shape[1]
    own_rows = 2 // lax.axis_size("tensor")
    gain_vector = norm_gain[0]
    value_matrix = value_weight[0]
    output_matrix = output_weight[0]
    saved_inputs = hidden_in[0]
    saved_pattern = attention_probs[0]
    positions = jnp.arange(sequence_length, dtype=jnp.int32)
    response_bool = (positions[None, None, :] >= sequence_bounds[:, 0:1, None]) & (
        positions[None, None, :] < sequence_bounds[:, 1:3, None]
    )
    response_mask = response_bool.astype(jnp.float32)
    sequence_logprob = jnp.sum(response_mask * policy_logprob, axis=-1)
    margin = DPO_BETA * (
        sequence_logprob[:, 0]
        - reference_logprob[:, 0]
        - (sequence_logprob[:, 1] - reference_logprob[:, 1])
    )
    weight_pair = jax.nn.sigmoid(-margin)
    local_count = jnp.sum(response_bool[:, 0, :].astype(jnp.int32))
    chosen_total = lax.psum(local_count, "dp")
    pair_total = micro_count * lax.axis_size("dp")
    likelihood_scale = (
        LIKELIHOOD_COEF * jnp.asarray(pair_total, jnp.float32) / chosen_total.astype(jnp.float32)
    )
    chosen_weight = (
        -DPO_BETA * weight_pair[:, None] * response_mask[:, 0]
        - likelihood_scale * response_mask[:, 0]
    )
    rejected_weight = DPO_BETA * weight_pair[:, None] * response_mask[:, 1]
    token_weight = jnp.stack([chosen_weight, rejected_weight], axis=1)
    full_head_grad = lax.all_gather(head_grad, "tensor", axis=1, tiled=True)
    top_cotangent = (token_weight[..., None] * full_head_grad.astype(jnp.float32)).astype(
        jnp.bfloat16
    )
    send_rows = 2

    def local_backward(operands):
        inputs, pattern, upstream = operands
        input_float = inputs.astype(jnp.float32)
        inverse_rms = lax.rsqrt(
            jnp.mean(input_float * input_float, axis=-1, keepdims=True) + EPSILON
        )
        normed = (input_float * inverse_rms * gain_vector).astype(jnp.bfloat16)
        values = jnp.dot(normed, value_matrix, preferred_element_type=jnp.float32).astype(
            jnp.bfloat16
        )
        grouped = pattern.reshape(2, value_heads, group_size, sequence_length, sequence_length)
        values_heads = values.reshape(2, sequence_length, value_heads, HEAD_DIM)
        mixed = jnp.einsum(
            "ckgst,ctke->cskge", grouped, values_heads, preferred_element_type=jnp.float32
        )
        mixed = mixed.astype(jnp.bfloat16).reshape(2, sequence_length, mixed_columns)
        mixed_grad = jnp.einsum(
            "csd,hd->csh", upstream, output_matrix, preferred_element_type=jnp.float32
        ).astype(jnp.bfloat16)
        mixed_heads = mixed_grad.reshape(2, sequence_length, value_heads, group_size, HEAD_DIM)
        values_grad = jnp.einsum(
            "ckgst,cskge->ctke", grouped, mixed_heads, preferred_element_type=jnp.float32
        )
        values_grad = values_grad.astype(jnp.bfloat16).reshape(2, sequence_length, value_columns)
        partial_value = jnp.einsum(
            "csk,dk->csd", values_grad, value_matrix, preferred_element_type=jnp.float32
        )
        return (partial_value, inverse_rms, normed, mixed, values_grad)

    def skipped(operands):
        return (
            jnp.zeros((2, sequence_length, model_width), jnp.float32),
            jnp.zeros((2, sequence_length, 1), jnp.float32),
            jnp.zeros((2, sequence_length, model_width), jnp.bfloat16),
            jnp.zeros((2, sequence_length, mixed_columns), jnp.bfloat16),
            jnp.zeros((2, sequence_length, value_columns), jnp.bfloat16),
        )

    def place(buffer, value, slot_index, active):
        previous = lax.dynamic_index_in_dim(buffer, slot_index, 0, keepdims=False)
        return lax.dynamic_update_index_in_dim(
            buffer, jnp.where(active, value, previous), slot_index, 0
        )

    def turn_step(turn, state_tuple):
        outgoing, outputs, gain_total, kept_state = state_tuple
        incoming = shifted(outgoing, "pipe", -1)
        micro_index = turn - (section_count - 1 - section_index)
        active = (micro_index >= 0) & (micro_index < micro_count)
        slot_index = jnp.clip(micro_index, 0, micro_count - 1)
        top_slice = lax.dynamic_index_in_dim(top_cotangent, slot_index, 0, keepdims=False)
        upstream = jnp.where(section_index == section_count - 1, top_slice, incoming)
        inputs = lax.dynamic_index_in_dim(saved_inputs, slot_index, 0, keepdims=False)
        pattern = lax.dynamic_index_in_dim(saved_pattern, slot_index, 0, keepdims=False)
        partial_value, inverse_rms, normed, mixed, values_grad = lax.cond(
            active, local_backward, skipped, (inputs, pattern, upstream)
        )
        normed_grad = over_copies(partial_value.astype(jnp.bfloat16), "tensor").astype(jnp.float32)
        input_float = inputs.astype(jnp.float32)
        scaled = normed_grad * gain_vector
        cubed = inverse_rms * inverse_rms * inverse_rms
        input_grad = inverse_rms * scaled - input_float * cubed * jnp.mean(
            input_float * scaled, axis=-1, keepdims=True
        )
        new_rows = (upstream.astype(jnp.float32) + input_grad).astype(jnp.bfloat16)
        gain_terms = jnp.sum(normed_grad * input_float * inverse_rms, axis=(0, 1))
        gain_total = gain_total + jnp.where(active, gain_terms, 0.0)
        outputs = place(outputs, new_rows, slot_index, active)
        saved_upstream, saved_mixed, saved_normed, saved_values = kept_state
        kept_state = (
            place(saved_upstream, upstream, slot_index, active),
            place(saved_mixed, mixed, slot_index, active),
            place(saved_normed, normed, slot_index, active),
            place(saved_values, values_grad, slot_index, active),
        )
        return (new_rows, outputs, gain_total, kept_state)

    kept_state = (
        jnp.zeros((micro_count, 2, sequence_length, model_width), jnp.bfloat16),
        jnp.zeros((micro_count, 2, sequence_length, mixed_columns), jnp.bfloat16),
        jnp.zeros((micro_count, 2, sequence_length, model_width), jnp.bfloat16),
        jnp.zeros((micro_count, 2, sequence_length, value_columns), jnp.bfloat16),
    )
    initial = (
        jnp.zeros((send_rows, sequence_length, model_width), jnp.bfloat16),
        jnp.zeros((micro_count, send_rows, sequence_length, model_width), jnp.bfloat16),
        jnp.zeros((model_width,), jnp.float32),
        kept_state,
    )
    final_state = lax.fori_loop(0, section_count + micro_count - 1, turn_step, initial)
    outgoing, outputs, gain_total, kept_state = final_state
    own_output = lax.dynamic_slice_in_dim(outputs, tensor_index * own_rows, own_rows, 1)
    saved_upstream, saved_mixed, saved_normed, saved_values = kept_state
    value_part = jnp.einsum(
        "mcsd,mcsk->dk", saved_normed, saved_values, preferred_element_type=jnp.float32
    )
    mixed_part = jnp.einsum(
        "mcsd,mcsh->dh", saved_upstream, saved_mixed, preferred_element_type=jnp.float32
    )
    grad_share = lax.psum_scatter(
        jnp.concatenate([value_part, mixed_part], axis=1), "dp", scatter_dimension=0, tiled=True
    )
    gain_rows = sent_and_summed(gain_total, "dp", 0)
    value_share = grad_share[:, :value_columns]
    mixed_share = grad_share[:, value_columns:]
    return (own_output[None], value_share[None], mixed_share[None], gain_rows[None])


def solution(mesh):
    in_specs = (
        P("pipe", "dp", None, None, None),
        P("pipe", "dp", None, "tensor", None, None),
        P("pipe", None),
        P("pipe", None, "tensor"),
        P("pipe", "tensor", None),
        P("dp", "tensor", None, None),
        P("dp", None, None),
        P("dp", None),
        P("dp", None),
    )
    out_specs = (
        P("pipe", "dp", "tensor", None, None),
        P("pipe", "dp", "tensor"),
        P("pipe", "dp", "tensor"),
        P("pipe", "dp"),
    )
    return jax.shard_map(body, mesh=mesh, in_specs=in_specs, out_specs=out_specs, check_vma=False)
```

profile of v0, /device:TPU:2, one launch (start us, length us, event | category | flops | bytes accessed | tf_op | source)
XLA Modules:
  0.0 610.0 jit_solution(3134515458669599194)
XLA Ops:
  11.1 27.1 %psum.7 = s32[]{:T(128)} all-reduce(s32[]{:T(128)} %fusion.36), channel_id=1, replica_groups=mesh['pipe'=2,'dp'=64,'tensor'=2] {'dp'}, use_global_device_ids=true, to_apply=%region_2.0 | all-reduce | flops 1 | bytes 8 | tf_op jit(solution)/shard_map/psum | solution.py:82
  38.8 2.0 copy.46
  41.2 7.4 %all-gather.2.cloned.1.call-done = bf16[2,2,64,3584]{3,2,1,0:T(8,128)(2,1)} async-done(((bf16[2,1,64,3584]{3,2,1,0:T(8,128)(2,1)}), bf16[2,2,64,3584]{3,2,1,0:T(8,128)(2,1)}) %all-gather.2.cloned.1.call-update) | async-done | bytes 1835024 | tf_op jit(solution)/shard_map/all_gather | solution.py:93
  48.6 3.2 multiply_convert_fusion
  56.8 156.4 %while.28 = (s32[]{:T(128)}, bf16[2,64,3584]{2,1,0:T(8,128)(2,1)}, bf16[2,2,64,3584]{3,2,1,0:T(8,128)(2,1)}, f32[3584]{0:T(1024)S(1)}, bf16[2,2,64,3584]{3,2,0,1...) while((s32[]{:T(128)}, bf16[2,64,3584]{2,1,0:T(8,128)(2,1)}, ...), condition=%wide.region_10.11_spmd.clone, body=%wide.region_3.10_spmd.clone.sunk | while | flops 1100947072 | bytes 85268616 | solution.py:188
  59.2 2.2 constant_dynamic-slice_fusion.13
  61.4 2.2 constant_dynamic-slice_fusion.11
  63.7 2.3 constant_dynamic-slice_fusion.10
  67.2 2.5 bitcast_dynamic-update-slice_fusion.10
  69.8 2.6 conditional.3
  72.4 2.5 broadcast_in_dim.114
  75.0 3.7 all-to-all-start
  79.5 2.3 bitcast_dynamic-update-slice_fusion.13
  81.8 12.8 %all-to-all-done = bf16[2,2,64,3584]{3,2,1,0:T(8,128)(2,1)S(1)} async-done(((bf16[2,2,64,3584]{3,2,1,0:T(8,128)(2,1)}), bf16[2,2,64,3584]{3,2,1,0:T(8,128)(2,1)S(1)}, u32[]{:S(2)}, u32[]{:S(2)}) %all-to-all-start) | async-done | bytes 1835040 | tf_op jit(solution)/shard_map/while/body/eval_jaxpr/all_to_all | solution.py:22
  96.8 2.2 bitcast_dynamic-update-slice_fusion.11
  102.6 2.2 constant_dynamic-slice_fusion.13
  104.8 2.2 constant_dynamic-slice_fusion.11
  107.0 2.3 constant_dynamic-slice_fusion.10
  110.6 1.9 collective-permute-done
  112.5 2.5 bitcast_dynamic-update-slice_fusion.10
  115.0 11.8 %conditional.3 = (bf16[2,64,3584]{2,1,0:T(8,128)(2,1)}, f32[2,64,1]{1,0,2:T(2,128)S(1)}, bf16[2,64,3584]{2,1,0:T(8,128)(2,1)}, bf16[2,64,896]{2,1,0:T(8,128)(2,1...) conditional(s32[]{:T(128)} %convert_element_type.173, () %tuple.76, ...), branch_computations={%region_4.4_spmd, %region_5.6_spmd} | conditional | flops 1089798656 | bytes 16857172 | solution.py:153
  115.0 5.0 fusion.9
  124.7 2.1 fusion.16
  126.8 2.5 broadcast_in_dim.114
  129.3 3.7 all-to-all-start
  134.6 2.6 bitcast_dynamic-update-slice_fusion.13
  137.2 15.1 %all-to-all-done = bf16[2,2,64,3584]{3,2,1,0:T(8,128)(2,1)S(1)} async-done(((bf16[2,2,64,3584]{3,2,1,0:T(8,128)(2,1)}), bf16[2,2,64,3584]{3,2,1,0:T(8,128)(2,1)S(1)}, u32[]{:S(2)}, u32[]{:S(2)}) %all-to-all-start) | async-done | bytes 1835040 | tf_op jit(solution)/shard_map/while/body/eval_jaxpr/all_to_all | solution.py:22
  154.5 2.2 bitcast_dynamic-update-slice_fusion.11
  160.2 2.2 constant_dynamic-slice_fusion.13
  162.4 2.2 constant_dynamic-slice_fusion.11
  164.7 2.3 constant_dynamic-slice_fusion.10
  168.3 2.5 bitcast_dynamic-update-slice_fusion.10
  170.8 11.8 %conditional.3 = (bf16[2,64,3584]{2,1,0:T(8,128)(2,1)}, f32[2,64,1]{1,0,2:T(2,128)S(1)}, bf16[2,64,3584]{2,1,0:T(8,128)(2,1)}, bf16[2,64,896]{2,1,0:T(8,128)(2,1...) conditional(s32[]{:T(128)} %convert_element_type.173, () %tuple.76, ...), branch_computations={%region_4.4_spmd, %region_5.6_spmd} | conditional | flops 1089798656 | bytes 16857172 | solution.py:153
  170.8 5.0 fusion.9
  180.5 2.1 fusion.16
  182.6 2.5 broadcast_in_dim.114
  185.1 3.7 all-to-all-start
  190.4 2.6 bitcast_dynamic-update-slice_fusion.13
  193.0 15.8 %all-to-all-done = bf16[2,2,64,3584]{3,2,1,0:T(8,128)(2,1)S(1)} async-done(((bf16[2,2,64,3584]{3,2,1,0:T(8,128)(2,1)}), bf16[2,2,64,3584]{3,2,1,0:T(8,128)(2,1)S(1)}, u32[]{:S(2)}, u32[]{:S(2)}) %all-to-all-start) | async-done | bytes 1835040 | tf_op jit(solution)/shard_map/while/body/eval_jaxpr/all_to_all | solution.py:22
  211.0 2.2 bitcast_dynamic-update-slice_fusion.11
  213.2 1.9 convolution_bitcast_fusion.2
  215.1 8.1 %convolution_bitcast_fusion.1 = f32[3584,896]{0,1:T(8,128)} fusion(bf16[2,2,64,3584]{3,2,0,1:T(8,128)(2,1)} %get-tuple-element.722, bf16[2,2,64,896]{3,2,0,1:T(8,128)(2,1)} %get-tuple-element.723), kind=kOutput, calls=%fused_computation.62 | convolution fusion | flops 1644167168 | bytes 15138816 | tf_op jit(solution)/shard_map/mcsd,mcsh->dh/dot_general | solution.py:195
  223.2 10.8 %pad_maximum_fusion = f32[3584,1024]{0,1:T(8,128)} fusion(f32[3584,896]{0,1:T(8,128)} %convolution_bitcast_fusion.1, f32[3584,128]{0,1:T(8,128)S(1)} %convolution_bitcast_fusion.2), kind=kLoop, calls=%fused_computation.61 | loop fusion | flops 3670016 | bytes 29360128 | tf_op jit(solution)/shard_map/concatenate | solution.py:199
  234.0 15.3 %copy.59 = f32[3584,1024]{1,0:T(8,128)} copy(f32[3584,1024]{0,1:T(8,128)} %pad_maximum_fusion) | data formatting | bytes 29360128
  250.1 11.5 %all-to-all-start.1 = ((f32[64,1,56]{2,1,0:T(1,128)}), f32[64,1,56]{2,1,0:T(1,128)S(1)}, u32[]{:S(2)}, u32[]{:S(2)}) async-start(f32[64,1,56]{2,1,0:T(1,128)} %bitcast.24), calls=%async_computation.1 | async-start | bytes 65536 | tf_op jit(solution)/shard_map/all_to_all | solution.py:37
  261.6 2.2 dynamic-slice_bitcast_fusion.1
  263.8 7.3 %all-to-all-done.1 = f32[64,1,56]{2,1,0:T(1,128)S(1)} async-done(((f32[64,1,56]{2,1,0:T(1,128)}), f32[64,1,56]{2,1,0:T(1,128)S(1)}, u32[]{:S(2)}, u32[]{:S(2)}) %all-to-all-start.1) | async-done | bytes 14368 | tf_op jit(solution)/shard_map/all_to_all | solution.py:37
  271.6 328.0 %reduce-scatter.4.cloned.1.call-done = f32[56,1024]{1,0:T(8,128)} async-done(((f32[3584,1024]{1,0:T(8,128)}), f32[56,1024]{1,0:T(8,128)}) %reduce-scatter.4.cloned.1.call-update) | async-done | bytes 229392
  (133 shorter events, 49.5 us)
Async XLA Ops:
  7.2 33.7 %copy-start.8 = (f32[2,2]{1,0:T(2,128)S(1)}, f32[2,2]{1,0:T(2,128)}, u32[]{:S(2)}) copy-start(f32[2,2]{1,0:T(2,128)} %param.20) | copy-start | bytes 52
  7.2 41.4 %all-gather.2.cloned.1.call-start = ((), (), s32[]{:S(2)}) async-start(), calls=%async_computation.3 | async-start | bytes 2752512 | tf_op jit(solution)/shard_map/all_gather | solution.py:93
  7.9 591.7 %reduce-scatter.4.cloned.1.call-start = ((), (), s32[]{:S(2)}) async-start(), calls=%async_computation.4 | async-start | bytes 14909440
  54.0 2.8 copy-start.1
  54.0 2.8 copy-start.7
  56.9 10.3 %collective-permute-start = (bf16[2,64,3584]{2,1,0:T(8,128)(2,1)S(1)}, bf16[2,64,3584]{2,1,0:T(8,128)(2,1)}, u32[]{:S(2)}, u32[]{:S(2)}) collective-permute-start(bf16[2,64,3584]{2,1,0:T(8,128)(2,1)S(1)} %broadcast_select_fusion.2), channel_id=1, source_target_pairs={{128,0},{129,1},{130,2},{131,3},{132,4},{133,5},{134,6},{135,7},{1... | collective-permute-start | bytes 2752520 | tf_op jit(solution)/shard_map/while/body/eval_jaxpr/ppermute | solution.py:17
  63.6 3.6 copy-start.4
  63.6 3.6 copy-start.5
  75.0 19.6 %all-to-all-start = ((bf16[2,2,64,3584]{3,2,1,0:T(8,128)(2,1)}), bf16[2,2,64,3584]{3,2,1,0:T(8,128)(2,1)S(1)}, u32[]{:S(2)}, u32[]{:S(2)}) async-start(bf16[2,2,64,3584]{3,2,1,0:T(8,128)(2,1)} %broadcast_in_dim.114), calls=%async_computation | async-start | bytes 3670016 | tf_op jit(solution)/shard_map/while/body/eval_jaxpr/all_to_all | solution.py:22
  94.6 1.5 copy-start
  94.9 1.9 copy-start.3
  96.8 2.2 copy-start.2
  100.3 12.2 %collective-permute-start = (bf16[2,64,3584]{2,1,0:T(8,128)(2,1)S(1)}, bf16[2,64,3584]{2,1,0:T(8,128)(2,1)}, u32[]{:S(2)}, u32[]{:S(2)}) collective-permute-start(bf16[2,64,3584]{2,1,0:T(8,128)(2,1)S(1)} %broadcast_select_fusion.2), channel_id=1, source_target_pairs={{128,0},{129,1},{130,2},{131,3},{132,4},{133,5},{134,6},{135,7},{1... | collective-permute-start | bytes 2752520 | tf_op jit(solution)/shard_map/while/body/eval_jaxpr/ppermute | solution.py:17
  107.0 5.5 copy-start.4
  107.0 5.5 copy-start.5
  115.0 5.0 copy-start.6
  129.3 22.9 %all-to-all-start = ((bf16[2,2,64,3584]{3,2,1,0:T(8,128)(2,1)}), bf16[2,2,64,3584]{3,2,1,0:T(8,128)(2,1)S(1)}, u32[]{:S(2)}, u32[]{:S(2)}) async-start(bf16[2,2,64,3584]{3,2,1,0:T(8,128)(2,1)} %broadcast_in_dim.114), calls=%async_computation | async-start | bytes 3670016 | tf_op jit(solution)/shard_map/while/body/eval_jaxpr/all_to_all | solution.py:22
  152.3 1.5 copy-start
  152.6 1.9 copy-start.3
  154.4 2.2 copy-start.2
  157.9 10.3 %collective-permute-start = (bf16[2,64,3584]{2,1,0:T(8,128)(2,1)S(1)}, bf16[2,64,3584]{2,1,0:T(8,128)(2,1)}, u32[]{:S(2)}, u32[]{:S(2)}) collective-permute-start(bf16[2,64,3584]{2,1,0:T(8,128)(2,1)S(1)} %broadcast_select_fusion.2), channel_id=1, source_target_pairs={{128,0},{129,1},{130,2},{131,3},{132,4},{133,5},{134,6},{135,7},{1... | collective-permute-start | bytes 2752520 | tf_op jit(solution)/shard_map/while/body/eval_jaxpr/ppermute | solution.py:17
  164.7 3.6 copy-start.4
  164.7 3.6 copy-start.5
  170.8 5.0 copy-start.6
  185.1 23.7 %all-to-all-start = ((bf16[2,2,64,3584]{3,2,1,0:T(8,128)(2,1)}), bf16[2,2,64,3584]{3,2,1,0:T(8,128)(2,1)S(1)}, u32[]{:S(2)}, u32[]{:S(2)}) async-start(bf16[2,2,64,3584]{3,2,1,0:T(8,128)(2,1)} %broadcast_in_dim.114), calls=%async_computation | async-start | bytes 3670016 | tf_op jit(solution)/shard_map/while/body/eval_jaxpr/all_to_all | solution.py:22
  208.8 1.5 copy-start
  209.1 1.9 copy-start.3
  211.0 2.2 copy-start.2
  250.1 20.9 %all-to-all-start.1 = ((f32[64,1,56]{2,1,0:T(1,128)}), f32[64,1,56]{2,1,0:T(1,128)S(1)}, u32[]{:S(2)}, u32[]{:S(2)}) async-start(f32[64,1,56]{2,1,0:T(1,128)} %bitcast.24), calls=%async_computation.1 | async-start | bytes 65536 | tf_op jit(solution)/shard_map/all_to_all | solution.py:37
Sparse Core Ops, SparseCore 0:
  9.8 38.7 all-gather.1
  249.5 350.0 reduce-scatter.3
where the time goes:
time: 615 us; the launch traced here: 610 us
  waiting for transfers between devices  389 us (63%)
  local copies, waits for them, and re-layouts  72 us (12%)
  other arithmetic  50.6 us (8%)
  matrix products  29.5 us (5%)
  blocking collectives  27.1 us (4%)
  starting transfers between devices  26.6 us (4%)
  between operations  14.8 us (2%)
    unnamed x3, waiting for transfers between devices  329 us
    all_to_all x3, waiting for transfers between devices, copy_for_each(): return lax.all_to_all(copies, axis, split_axis=0, concat_axis=0, tiled=True)  43.7 us
    psum x1, blocking collectives, body(): chosen_total = lax.psum(local_count, 'dp')  27.1 us
    dynamic_update_slice x15, other arithmetic, place(): lax.dynamic_update_index_in_dim(buffer, jnp.where(active, value, previous...  25.6 us
    dynamic_slice x15, local copies, waits for them, and re-layouts, place(): previous = lax.dynamic_index_in_dim(buffer, slot_index, 0, keepdims=False)  23.1 us
    unnamed x12, local copies, waits for them, and re-layouts  19.2 us
  transfers between devices with their start and end apart: 9, of which 7 were waited for; matrix products, arithmetic and copies ran while one was open for 8% of the time, Pallas kernels for 0%

commit v1 on v0

v1 whole, which is shorter than its diff:
```python
import functools

import jax
import jax.numpy as jnp
from jax import lax
from jax.experimental import pallas as pl
from jax.experimental.pallas import tpu as pltpu
from jax.sharding import PartitionSpec as P

HEAD_DIM = 128
EPSILON = 1e-06
DPO_BETA = 0.25
LIKELIHOOD_COEF = 0.2
MESH = pl.DeviceIdType.MESH
BF = jnp.bfloat16
F32 = jnp.float32
COLS = 512


class Flow:
    def __init__(self, size, place, ahead, behind, local, landing, sends, receives, base, hops):
        self.size, self.place = size, place
        self.target = {1: ahead, -1: behind}
        self.local, self.landing = local, landing
        self.sends, self.receives = sends, receives
        self.hops = hops
        self.slot = {}
        for (way, half), count in hops.items():
            for step in range(count):
                self.slot[way, half, step] = base + len(self.slot)
        self.count = len(self.slot)
        self.copies = {}

    def copy(self, way, half, step):
        slot = self.slot[way, half, step]
        chunk = lax.rem(self.place + way * (self.hops[way, half] - step) + self.size, self.size)
        return chunk, pltpu.make_async_remote_copy(
            src_ref=self.local(chunk, half),
            dst_ref=self.landing(slot),
            send_sem=self.sends.at[slot],
            recv_sem=self.receives.at[slot],
            device_id=self.target[way],
            device_id_type=MESH,
        )

    def collect(self, way, half, step, chunk):
        self.copies[way, half, step].wait_recv()
        target = self.local(chunk, half)
        landed = self.landing(self.slot[way, half, step])
        add_into(target, landed)

    def step(self, step):
        for way, half in self.hops:
            if step < self.hops[way, half]:
                chunk, copy = self.copy(way, half, step)
                if step:
                    self.collect(way, half, step - 1, chunk)
                copy.start()
                self.copies[way, half, step] = copy

    def finish(self):
        for (way, half), count in self.hops.items():
            self.collect(way, half, count - 1, self.place)

    def drain(self):
        for copy in self.copies.values():
            copy.wait_send()


def add_into(target, landed):
    if len(target.shape) > 2 and target.shape[-2] > 1:

        def one(index, carry):
            target[index] = target[index] + landed[index]
            return carry

        lax.fori_loop(0, target.shape[0], one, 0)
    else:
        target[...] = target[...] + landed[...]


def scatter_kernel(
    mixed_hbm,
    value_hbm,
    gain_hbm,
    mixed_out,
    value_out,
    gain_out,
    part_a,
    part_b,
    part_g,
    land_a1,
    land_b1,
    land_a2,
    land_b2,
    land_g1,
    land_g2,
    last_src,
    last_dst,
    last_g,
    load_sems,
    sends,
    receives,
):
    pipe = lax.axis_index("pipe")
    tensor = lax.axis_index("tensor")
    dp = lax.axis_index("dp")
    z = dp // 8
    y = lax.rem(dp, 8) // 2
    x = lax.rem(dp, 2)

    def device(z_at, y_at, x_at):
        return (pipe, z_at * 8 + y_at * 2 + x_at, tensor)

    z_next, z_prev = lax.rem(z + 1, 8), lax.rem(z + 7, 8)
    y_next, y_prev = lax.rem(y + 1, 4), lax.rem(y + 3, 4)
    z_ways = (device(z_next, y, x), device(z_prev, y, x))
    y_ways = (device(z, y_next, x), device(z, y_prev, x))
    x_way = device(z, y, 1 - x)
    loads = [
        pltpu.make_async_copy(mixed_hbm.at[:, :, :, pl.ds(0, COLS)], part_a, load_sems.at[0]),
        pltpu.make_async_copy(
            mixed_hbm.at[:, :, :, pl.ds(COLS, COLS - HEAD_DIM)],
            part_b.at[:, :, :, pl.ds(0, COLS - HEAD_DIM)],
            load_sems.at[1],
        ),
        pltpu.make_async_copy(
            value_hbm, part_b.at[:, :, :, pl.ds(COLS - HEAD_DIM, HEAD_DIM)], load_sems.at[2]
        ),
        pltpu.make_async_copy(gain_hbm, part_g, load_sems.at[3]),
    ]
    for load in loads:
        load.start()
    barrier = pltpu.get_barrier_semaphore()
    for neighbour in (*z_ways, *y_ways, x_way):
        pl.semaphore_signal(barrier, inc=1, device_id=neighbour, device_id_type=MESH)
    pl.semaphore_wait(barrier, 5)
    for load in loads:
        load.wait()

    base = 0

    def flow(size, place, ways, local, landing, hops):
        nonlocal base
        first = base
        made = Flow(
            size, place, *ways, local, lambda slot: landing.at[slot - first], sends, receives, base, hops
        )
        base += made.count
        return made

    z_halves = {(1, 0): 4, (-1, 1): 4, (1, 1): 3, (-1, 0): 3}
    y_halves = {(1, 0): 2, (-1, 1): 2, (1, 1): 1, (-1, 0): 1}
    z_whole = {(1, 0): 4, (-1, 0): 3}
    y_whole = {(1, 0): 2, (-1, 0): 1}
    a1 = flow(8, z, z_ways, lambda q, h: part_a.at[q, pl.ds(2 * h, 2)], land_a1, z_halves)
    b1 = flow(4, y, y_ways, lambda q, h: part_b.at[pl.ds(4 * h, 4), q], land_b1, y_halves)
    a2 = flow(4, y, y_ways, lambda q, h: part_a.at[z, q], land_a2, y_whole)
    b2 = flow(8, z, z_ways, lambda q, h: part_b.at[q, y], land_b2, z_whole)
    g1 = flow(8, z, z_ways, lambda q, h: part_g.at[q], land_g1, z_whole)
    g2 = flow(4, y, y_ways, lambda q, h: part_g.at[z, q], land_g2, y_whole)

    def last(index, source, target):
        return pltpu.make_async_remote_copy(
            src_ref=source,
            dst_ref=target,
            send_sem=sends.at[base + index],
            recv_sem=receives.at[base + index],
            device_id=x_way,
            device_id_type=MESH,
        )

    def exchange(index, part):
        total = part[z, y].astype(F32)
        low, high = total[:56], total[56:]
        last_src[index] = jnp.where(x == 0, high, low).astype(BF)
        copy = last(index, last_src.at[index], last_dst.at[index])
        copy.start()
        return copy, jnp.where(x == 0, low, high)

    a1.step(0)
    b1.step(0)
    g1.step(0)
    a1.step(1)
    b1.step(1)
    g1.step(1)
    a1.step(2)
    g1.step(2)
    a1.step(3)
    g1.step(3)
    b1.finish()
    b2.step(0)
    a1.finish()
    a2.step(0)
    g1.finish()
    g2.step(0)
    b2.step(1)
    a2.step(1)
    g2.step(1)
    b2.step(2)
    a2.finish()
    copy_a, own_a = exchange(0, part_a)
    mixed_out[:, :COLS] = own_a
    g2.finish()
    copy_g = last(2, part_g.at[z, y], last_g)
    copy_g.start()
    b2.step(3)
    b2.finish()
    copy_b, own_b = exchange(1, part_b)
    mixed_out[:, COLS:] = own_b[:, : COLS - HEAD_DIM]
    value_out[...] = own_b[:, COLS - HEAD_DIM :]
    copy_a.wait_recv()
    mixed_out[:, :COLS] += last_dst[0].astype(F32)
    copy_g.wait_recv()
    gain_out[...] = part_g[z, y] + last_g[...]
    copy_b.wait_recv()
    landed = last_dst[1].astype(F32)
    mixed_out[:, COLS:] += landed[:, : COLS - HEAD_DIM]
    value_out[...] += landed[:, COLS - HEAD_DIM :]
    for made in (a1, b1, a2, b2, g1, g2):
        made.drain()
    for copy in (copy_a, copy_b, copy_g):
        copy.wait_send()


def reduce_scatter(mixed_part, value_part, gain_part):
    width = mixed_part.shape[1]
    copies = 14 + 6 + 3 + 7 + 7 + 3 + 3
    vmem = pl.BlockSpec(memory_space=pltpu.VMEM)
    hbm = pl.BlockSpec(memory_space=pl.ANY)
    gain_rows = jnp.pad(gain_part.reshape(8, 4, 1, 112), ((0, 0), (0, 0), (0, 0), (0, 16)))
    return pl.pallas_call(
        scatter_kernel,
        out_shape=(
            jax.ShapeDtypeStruct((56, width), F32),
            jax.ShapeDtypeStruct((56, HEAD_DIM), F32),
            jax.ShapeDtypeStruct((1, 128), F32),
        ),
        in_specs=[hbm, hbm, hbm],
        out_specs=(vmem, vmem, vmem),
        scratch_shapes=[
            pltpu.VMEM((8, 4, 112, COLS), BF),
            pltpu.VMEM((8, 4, 112, COLS), BF),
            pltpu.VMEM((8, 4, 1, 128), F32),
            pltpu.VMEM((14, 2, 112, COLS), BF),
            pltpu.VMEM((6, 4, 112, COLS), BF),
            pltpu.VMEM((3, 112, COLS), BF),
            pltpu.VMEM((7, 112, COLS), BF),
            pltpu.VMEM((7, 4, 1, 128), F32),
            pltpu.VMEM((3, 1, 128), F32),
            pltpu.VMEM((2, 56, COLS), BF),
            pltpu.VMEM((2, 56, COLS), BF),
            pltpu.VMEM((1, 128), F32),
            pltpu.SemaphoreType.DMA((4,)),
            pltpu.SemaphoreType.DMA((copies,)),
            pltpu.SemaphoreType.DMA((copies,)),
        ],
        compiler_params=pltpu.CompilerParams(
            collective_id=0, has_side_effects=True, vmem_limit_bytes=40 * 1024 * 1024
        ),
    )(
        mixed_part.reshape(8, 4, 112, width),
        value_part.reshape(8, 4, 112, HEAD_DIM),
        gain_rows,
    )


def body(
    hidden_in,
    attention_probs,
    norm_gain,
    value_weight,
    output_weight,
    head_grad,
    policy_logprob,
    reference_logprob,
    sequence_bounds,
):
    section = lax.axis_index("pipe")
    tensor_index = lax.axis_index("tensor")
    pairs, _, length, width = hidden_in.shape[1:]
    tokens = pairs * 2 * length
    heads = attention_probs.shape[3]
    gain_vector = norm_gain[0]
    value_matrix = value_weight[0]
    output_matrix = output_weight[0]
    pattern = attention_probs[0].reshape(pairs * 2, heads, length, length)
    inputs = hidden_in[0].reshape(tokens, width)

    other_head = lax.ppermute(head_grad, ("pipe", "tensor"), [(2, 3), (3, 2)])
    other_matrix = lax.ppermute(value_matrix, "tensor", [(0, 1), (1, 0)])

    positions = jnp.arange(length, dtype=jnp.int32)
    response_bool = (positions[None, None, :] >= sequence_bounds[:, 0:1, None]) & (
        positions[None, None, :] < sequence_bounds[:, 1:3, None]
    )
    response_mask = response_bool.astype(F32)
    sequence_logprob = jnp.sum(response_mask * policy_logprob, axis=-1)
    margin = DPO_BETA * (
        sequence_logprob[:, 0]
        - reference_logprob[:, 0]
        - (sequence_logprob[:, 1] - reference_logprob[:, 1])
    )
    weight_pair = jax.nn.sigmoid(-margin)
    local_count = jnp.sum(response_bool[:, 0, :].astype(jnp.int32))
    chosen_total = lax.psum(local_count, "dp")
    pair_total = pairs * lax.axis_size("dp")
    likelihood_scale = (
        LIKELIHOOD_COEF * jnp.asarray(pair_total, F32) / chosen_total.astype(F32)
    )
    chosen_weight = (
        -DPO_BETA * weight_pair[:, None] * response_mask[:, 0]
        - likelihood_scale * response_mask[:, 0]
    )
    rejected_weight = DPO_BETA * weight_pair[:, None] * response_mask[:, 1]
    token_weight = jnp.stack([chosen_weight, rejected_weight], axis=1)

    input_float = inputs.astype(F32)
    inverse_rms = lax.rsqrt(jnp.mean(input_float * input_float, axis=-1, keepdims=True) + EPSILON)
    normed = (input_float * inverse_rms * gain_vector).astype(BF)
    values = jnp.dot(normed, value_matrix, preferred_element_type=F32).astype(BF)
    values = values.reshape(pairs * 2, length, HEAD_DIM)
    mixed = jnp.einsum("nhqk,nke->nqhe", pattern, values, preferred_element_type=F32)
    mixed = mixed.astype(BF).reshape(tokens, heads * HEAD_DIM)

    def through(upstream):
        mixed_grad = jnp.einsum(
            "nd,hd->nh", upstream, output_matrix, preferred_element_type=F32
        ).astype(BF)
        mixed_heads = mixed_grad.reshape(pairs * 2, length, heads, HEAD_DIM)
        values_grad = jnp.einsum(
            "nhqk,nqhe->nke", pattern, mixed_heads, preferred_element_type=F32
        )
        values_grad = values_grad.astype(BF).reshape(tokens, HEAD_DIM)
        other_grad = lax.ppermute(values_grad, "tensor", [(0, 1), (1, 0)])
        normed_grad = jnp.einsum(
            "nk,dk->nd", values_grad, value_matrix, preferred_element_type=F32
        ).astype(BF).astype(F32) + jnp.einsum(
            "nk,dk->nd", other_grad, other_matrix, preferred_element_type=F32
        ).astype(BF).astype(F32)
        scaled = normed_grad * gain_vector
        cubed = inverse_rms * inverse_rms * inverse_rms
        input_grad = inverse_rms * scaled - input_float * cubed * jnp.mean(
            input_float * scaled, axis=-1, keepdims=True
        )
        below = (upstream.astype(F32) + input_grad).astype(BF)
        gain_terms = jnp.sum(normed_grad * input_float * inverse_rms, axis=0)
        return below, gain_terms, values_grad

    both = jnp.where(
        tensor_index == 0,
        jnp.concatenate([head_grad, other_head], axis=1),
        jnp.concatenate([other_head, head_grad], axis=1),
    )
    top = (token_weight[..., None] * both.astype(F32)).astype(BF).reshape(tokens, width)
    below_top, _, _ = through(top)
    passed = lax.ppermute(below_top, "pipe", [(1, 0)])
    upstream = jnp.where(section == 1, top, passed)
    below, gain_terms, values_grad = through(upstream)
    own_output = lax.dynamic_slice_in_dim(
        below.reshape(pairs, 2, length, width), tensor_index, 1, 1
    )
    value_part = jnp.einsum("nd,nk->dk", normed, values_grad, preferred_element_type=F32)
    mixed_part = jnp.einsum("nd,nh->dh", upstream, mixed, preferred_element_type=F32)
    mixed_share, value_share, gain_share = reduce_scatter(
        mixed_part.astype(BF), value_part.astype(BF), gain_terms
    )
    x = lax.rem(lax.axis_index("dp"), 2)
    gain_rows = lax.dynamic_slice_in_dim(gain_share[0], x * 56, 56, 0)
    return (own_output[None], value_share[None], mixed_share[None], gain_rows[None])


def solution(mesh):
    in_specs = (
        P("pipe", "dp", None, None, None),
        P("pipe", "dp", None, "tensor", None, None),
        P("pipe", None),
        P("pipe", None, "tensor"),
        P("pipe", "tensor", None),
        P("dp", "tensor", None, None),
        P("dp", None, None),
        P("dp", None),
        P("dp", None),
    )
    out_specs = (
        P("pipe", "dp", "tensor", None, None),
        P("pipe", "dp", "tensor"),
        P("pipe", "dp", "tensor"),
        P("pipe", "dp"),
    )
    return jax.shard_map(body, mesh=mesh, in_specs=in_specs, out_specs=out_specs, check_vma=False)
```

time: 615 us -> 177 us (0.29)
  waiting for transfers between devices: 389 us -> 8.73 us
  Pallas kernels: 0 us -> 57.8 us
  local copies, waits for them, and re-layouts: 72 us -> 15.9 us
  other arithmetic: 50.6 us -> 16 us
  starting transfers between devices: 26.6 us -> 6.74 us
  blocking collectives: 27.1 us -> 40.5 us
  between operations: 14.8 us -> 1.63 us
    unnamed x3 -> x0, waiting for transfers between devices: 329 us -> none
    pallas_call x0 -> x1, Pallas kernels: none -> 57.8 us  [reduce_scatter(): pl.pallas_call(scatter_kernel, out_shape=(jax.ShapeDtypeStruct((56, width...]
    all_to_all x4 -> x0, waiting for transfers between devices: 51 us -> none  [the longest x3 43.7 us: copy_for_each(): return lax.all_to_all(copies, axis, split_axis=0, concat_axis=0, tiled=True)]
    dynamic_update_slice x15 -> x0, other arithmetic: 25.6 us -> none  [place(): lax.dynamic_update_index_in_dim(buffer, jnp.where(active, value, previous...]
    all_to_all x4 -> x0, starting transfers between devices: 22.6 us -> none  [the longest x1 11.5 us: sent_and_summed(): parts = lax.all_to_all(split_up(shard, dim, length), axis, 0, 0, tiled=True)]
    dynamic_slice x15 -> x1, local copies, waits for them, and re-layouts: 23.1 us -> 0.58 us  [body(): gain_rows = lax.dynamic_slice_in_dim(gain_share[0], x * 56, 56, 0)]
    psum x1, blocking collectives: 27.1 us -> 40.5 us  [body(): chosen_total = lax.psum(local_count, 'dp')]
    unnamed x12 -> x28, local copies, waits for them, and re-layouts: 19.2 us -> 6.62 us
  transfers between devices with their start and end apart: 9 -> 5, of which waited for: 7 -> 2; matrix products, arithmetic and copies ran while one was open for 8% -> 16% of each run, Pallas kernels for 0% -> 0%
where the time goes in v1:
time: 177 us; the launch traced here: 176 us
  Pallas kernels  57.8 us (33%)
  blocking collectives  40.5 us (23%)
  matrix products  28.5 us (16%)
  other arithmetic  16 us (9%)
  local copies, waits for them, and re-layouts  15.9 us (9%)
  waiting for transfers between devices  8.73 us (5%)
  starting transfers between devices  6.74 us (4%)
    pallas_call x1, Pallas kernels, reduce_scatter(): pl.pallas_call(scatter_kernel, out_shape=(jax.ShapeDtypeStruct((56, width...  57.8 us
    psum x1, blocking collectives, body(): chosen_total = lax.psum(local_count, 'dp')  40.5 us
    dot_general x2, matrix products, through(): jnp.einsum('nd,hd->nh', upstream, output_matrix, preferred_element_type=F32)  11.5 us
    unnamed x28, local copies, waits for them, and re-layouts  6.62 us
    dot_general x2, matrix products, through(): jnp.einsum('nk,dk->nd', other_grad, other_matrix, preferred_element_type=...  6.52 us
    dot_general x1, matrix products, body(): jnp.einsum('nd,nh->dh', upstream, mixed, preferred_element_type=F32)  4.8 us
    reshape x2, local copies, waits for them, and re-layouts, through(): mixed_heads = mixed_grad.reshape(pairs * 2, length, heads, HEAD_DIM)  4.75 us
    ppermute x2, waiting for transfers between devices, through(): other_grad = lax.ppermute(values_grad, 'tensor', [(0, 1), (1, 0)])  4.72 us
  transfers between devices with their start and end apart: 5, of which 2 were waited for; matrix products, arithmetic and copies ran while one was open for 16% of the time, Pallas kernels for 0%

profile of v1, /device:TPU:2, one launch (start us, length us, event | category | flops | bytes accessed | tf_op | source)
XLA Modules:
  0.0 175.9 jit_solution(9670356439950267226)
XLA Ops:
  0.6 0.9 collective-permute-start
  1.5 2.2 %collective-permute-start.2 = (bf16[3584,128]{1,0:T(8,128)(2,1)}, bf16[3584,128]{1,0:T(8,128)(2,1)}, u32[]{:S(2)}, u32[]{:S(2)}) collective-permute-start(bf16[3584,128]{1,0:T(8,128)(2,1)} %bitcast.116), channel_id=1, source_target_pairs={{0,1},{1,0},{2,3},{3,2},{4,5},{5,4},{6,7},{7,6},{8,9},{9,8},{10,11... | collective-permute-start | bytes 2752520 | tf_op jit(solution)/shard_map/ppermute | solution.py:291
  3.7 0.7 slice.29
  4.5 0.8 slice_reduce_fusion
  5.3 0.8 select_reduce_fusion
  6.2 0.6 fusion.41
  6.8 1.9 %fusion.19 = f32[2,2,64]{2,1,0:T(2,128)S(1)} fusion(bf16[1,2,2,64,3584]{4,3,2,1,0:T(8,128)(2,1)} %param.9), kind=kLoop, calls=%fused_computation.31 | loop fusion | flops 2752256 | bytes 1836032 | tf_op jit(solution)/shard_map/reduce_sum | solution.py:319
  8.8 40.5 %psum.7 = s32[]{:T(128)} all-reduce(s32[]{:T(128)} %fusion.41), channel_id=1, replica_groups=mesh['pipe'=2,'dp'=64,'tensor'=2] {'dp'}, use_global_device_ids=true, to_apply=%region_2.0 | all-reduce | flops 1 | bytes 8 | tf_op jit(solution)/shard_map/psum | solution.py:306
  49.9 0.1 rsqrt.16
  50.1 1.0 multiply_reduce_fusion.1
  51.1 0.1 multiply_subtract_fusion
  51.1 0.1 mul.199
  51.2 0.8 reduce.5
  52.0 2.0 %multiply_convert_fusion = bf16[2,2,64,3584]{3,2,1,0:T(8,128)(2,1)S(1)} fusion(f32[2,2,64]{2,1,0:T(2,128)S(1)} %pad_maximum_fusion, bf16[2,1,64,3584]{3,2,1,0:T(8,128)(2,1)} %param.14, bf16[2,1,64,3584]{3,2,1,0:T(8,128)(2,1)S(1)} %collective-permute-done, pred[]{:T(512)S(6)} %eq.7), kind=kLoop, calls=%fused_computation.40 | loop fusion | flops 5505024 | bytes 3671041 | tf_op jit(solution)/shard_map/convert_element_type | solution.py:355
  54.0 5.8 %fusion.28 = bf16[256,896]{1,0:T(8,128)(2,1)} fusion(bf16[256,3584]{1,0:T(8,128)(2,1)S(1)} %bitcast.119, bf16[1,896,3584]{2,1,0:T(8,128)(2,1)} %param.13), kind=kOutput, calls=%fused_computation.44 | convolution fusion | flops 1644396544 | bytes 8716288 | tf_op jit(solution)/shard_map/nd,hd->nh/dot_general | solution.py:327
  59.8 2.4 %reshape.183 = bf16[4,64,7,128]{3,2,1,0:T(8,128)(2,1)} reshape(bf16[256,896]{1,0:T(8,128)(2,1)} %fusion.28) | data formatting | bytes 917504 | tf_op jit(solution)/shard_map/reshape | solution.py:330
  62.2 1.4 fusion.35
  63.6 0.1 collective-permute-start.1
  63.7 0.3 fusion.27
  64.1 0.6 fusion.10
  64.7 4.7 %collective-permute-done.1 = bf16[256,128]{1,0:T(8,128)(2,1)S(1)} collective-permute-done((bf16[256,128]{1,0:T(8,128)(2,1)S(1)}, bf16[256,128]{1,0:T(8,128)(2,1)S(1)}, u32[]{:S(2)}, u32[]{:S(2)}) %collective-permute-start.1) | collective-permute-done | bytes 65568 | tf_op jit(solution)/shard_map/ppermute | solution.py:335
  69.4 2.1 %fusion.22 = (f32[256]{0:T(256)S(1)}, f32[256,3584]{1,0:T(8,128)S(1)}) fusion(bf16[1,2,2,64,3584]{4,3,2,1,0:T(8,128)(2,1)S(1)} %copy-done.2, f32[3584]{0:T(1024)S(1)} %reduce.5, f32[256,3584]{1,0:T(8,128)S(1)} %fusion.10, bf16[256,128]{1,0:T(8,128)(2,1)S(1)} %collective-permute-done.1, bf16[3584,128]{1,0:T(8,128)(2,1)} %collective-permute-done.2), kind=kOutput, calls=%fused_computation.34 | convolution fusion | flops 241303296 | bytes 10173440 | tf_op jit(solution)/shard_map/nk,dk->nd/dot_general | solution.py:338
  71.6 3.1 %fusion.15 = bf16[256,3584]{1,0:T(8,128)(2,1)} fusion(bf16[1,2,2,64,3584]{4,3,2,1,0:T(8,128)(2,1)S(1)} %copy-done.2, f32[256,3584]{1,0:T(8,128)S(1)} %get-tuple-element.19, f32[256]{0:T(256)S(1)} %broadcast_multiply_fusion.1, f32[256]{0:T(256)S(1)} %multiply_multiply_fusion, f32[256]{0:T(256)S(1)} %rsqrt.16, f32[2,2,64,3584]{3,2,1,0:T(8,128)S(1)} %fusion.27, ...), kind=kLoop, calls=%fused_computation.27 | loop fusion | flops 9175040 | bytes 11014144 | tf_op jit(solution)/shard_map/convert_element_type | solution.py:346
  74.7 1.5 collective-permute-start.3
  76.2 0.5 fusion.21
  76.7 1.2 copy-done.7
  78.0 0.6 convolution_convert_fusion.7
  78.6 0.3 fusion.34
  78.9 1.1 copy.21
  80.0 4.0 %collective-permute-done.3 = bf16[256,3584]{1,0:T(8,128)(2,1)} collective-permute-done((bf16[256,3584]{1,0:T(8,128)(2,1)}, bf16[256,3584]{1,0:T(8,128)(2,1)}, u32[]{:S(2)}, u32[]{:S(2)}) %collective-permute-start.3) | collective-permute-done | bytes 1835040 | tf_op jit(solution)/shard_map/ppermute | solution.py:357
  84.0 3.2 %broadcast_select_fusion = bf16[256,3584]{1,0:T(8,128)(2,1)S(1)} fusion(bf16[256,3584]{1,0:T(8,128)(2,1)} %collective-permute-done.3, pred[]{:T(512)S(6)} %eq.6, f32[2,2,64,3584]{3,2,1,0:T(8,128)} %copy-done.3, f32[256]{0:T(256)S(1)} %mul.199), kind=kLoop, calls=%fused_computation.43 | loop fusion | flops 2752512 | bytes 7341057 | tf_op jit(solution)/shard_map/jit(_where)/select_n | solution.py:358
  87.2 1.2 copy-done.4
  88.5 5.7 %fusion.31 = bf16[256,896]{1,0:T(8,128)(2,1)} fusion(bf16[256,3584]{1,0:T(8,128)(2,1)S(1)} %broadcast_select_fusion, bf16[1,896,3584]{2,1,0:T(8,128)(2,1)} %param.13), kind=kOutput, calls=%fused_computation.45 | convolution fusion | flops 1644396544 | bytes 8716288 | tf_op jit(solution)/shard_map/nd,hd->nh/dot_general | solution.py:327
  94.2 2.3 %reshape.185 = bf16[4,64,7,128]{3,2,1,0:T(8,128)(2,1)} reshape(bf16[256,896]{1,0:T(8,128)(2,1)} %fusion.31) | data formatting | bytes 917504 | tf_op jit(solution)/shard_map/reshape | solution.py:330
  96.5 1.5 fusion.36
  98.1 0.6 fusion.6
  98.7 2.1 %collective-permute-start.4 = (bf16[256,128]{1,0:T(8,128)(2,1)S(1)}, bf16[256,128]{1,0:T(8,128)(2,1)S(1)}, u32[]{:S(2)}, u32[]{:S(2)}) collective-permute-start(bf16[256,128]{1,0:T(8,128)(2,1)S(1)} %bitcast.121), channel_id=1, source_target_pairs={{0,1},{1,0},{2,3},{3,2},{4,5},{5,4},{6,7},{7,6},{8,9},{9,8},{10,11... | collective-permute-start | bytes 196616 | tf_op jit(solution)/shard_map/ppermute | solution.py:335
  100.8 4.8 %convolution_convert_fusion = bf16[3584,896]{1,0:T(8,128)(2,1)} fusion(bf16[256,3584]{1,0:T(8,128)(2,1)S(1)} %copy-done.5, bf16[32,8,7,128]{3,2,1,0:T(8,128)(2,1)S(1)} %bitcast.118), kind=kOutput, calls=%fused_computation | convolution fusion | flops 1647378432 | bytes 8716288 | tf_op jit(solution)/shard_map/nd,nh->dh/dot_general | solution.py:364
  105.6 0.7 convolution_convert_fusion.5
  106.3 4.4 %fusion.25 = (f32[3584]{0:T(1024)S(1)}, f32[256]{0:T(256)S(1)}, f32[256,3584]{1,0:T(8,128)}) fusion(bf16[1,2,2,64,3584]{4,3,2,1,0:T(8,128)(2,1)S(1)} %copy-done.2, f32[256]{0:T(256)S(1)} %rsqrt.16, f32[3584]{0:T(1024)S(1)} %reduce.5, f32[256,3584]{1,0:T(8,128)S(1)} %fusion.6, bf16[256,128]{1,0:T(8,128)(2,1)S(1)} %collective-permute-done.4, ...), kind=kOutput, calls=%fused_computation.37 | convolution fusion | flops 244052224 | bytes 10188800 | tf_op jit(solution)/shard_map/nk,dk->nd/dot_general | solution.py:338
  110.7 0.1 reshape.192
  110.9 2.8 %copy-done.1 = bf16[3584,896]{1,0:T(8,128)(2,1)S(1)} copy-done((bf16[3584,896]{1,0:T(8,128)(2,1)S(1)}, bf16[3584,896]{1,0:T(8,128)(2,1)}, u32[]{:S(2)}) %copy-start.1) | copy-done | bytes 6422552
  113.7 57.8 %shard_map.120 = (f32[56,896]{1,0:T(8,128)S(1)}, f32[56,128]{1,0:T(8,128)S(1)}, f32[1,128]{1,0:T(1,128)S(1)}) custom-call(bf16[8,4,112,896]{3,2,1,0:T(8,128)(2,1)S(1)} %bitcast.110, bf16[8,4,112,128]{3,2,1,0:T(8,128)(2,1)S(1)} %bitcast.111, f32[8,4,1,128]{3,2,1,0:T(1,128)S(1)} %pad.4.gain_hbm), custom_call_target="tpu_custom_call" | custom-call | tf_op jit(solution)/shard_map/pallas_call | solution.py:232
  171.5 1.5 fusion.18
  173.0 1.0 dynamic-slice_bitcast_fusion
  174.0 0.6 constant_dynamic-slice_fusion
  174.6 0.6 copy.38
  175.2 0.7 copy.39
  (34 shorter events, 0.2 us)
Async XLA Ops:
  0.6 61.6 %copy-start = (bf16[1,2,2,7,64,64]{5,4,3,2,1,0:T(8,128)(2,1)S(1)}, bf16[1,2,2,7,64,64]{5,4,3,2,1,0:T(8,128)(2,1)}, u32[]{:S(2)}) copy-start(bf16[1,2,2,7,64,64]{5,4,3,2,1,0:T(8,128)(2,1)} %param.10) | copy-start | bytes 688132
  0.6 51.4 %collective-permute-start = (bf16[2,1,64,3584]{3,2,1,0:T(8,128)(2,1)}, bf16[2,1,64,3584]{3,2,1,0:T(8,128)(2,1)S(1)}, u32[]{:S(2)}, u32[]{:S(2)}) collective-permute-start(bf16[2,1,64,3584]{3,2,1,0:T(8,128)(2,1)} %param.14), channel_id=1, source_target_pairs={{128,129},{129,128},{130,131},{131,130},{132,133},{133,132},{134,1... | collective-permute-start | bytes 2752520 | tf_op jit(solution)/shard_map/ppermute | solution.py:290
  1.5 63.2 %collective-permute-start.2 = (bf16[3584,128]{1,0:T(8,128)(2,1)}, bf16[3584,128]{1,0:T(8,128)(2,1)}, u32[]{:S(2)}, u32[]{:S(2)}) collective-permute-start(bf16[3584,128]{1,0:T(8,128)(2,1)} %bitcast.116), channel_id=1, source_target_pairs={{0,1},{1,0},{2,3},{3,2},{4,5},{5,4},{6,7},{7,6},{8,9},{9,8},{10,11... | collective-permute-start | bytes 2752520 | tf_op jit(solution)/shard_map/ppermute | solution.py:291
  54.0 9.7 %copy-start.11 = (bf16[2,1,64,3584]{3,2,1,0:T(8,128)(2,1)S(1)}, bf16[2,1,64,3584]{3,2,1,0:T(8,128)(2,1)}, u32[]{:S(2)}) copy-start(bf16[2,1,64,3584]{3,2,1,0:T(8,128)(2,1)} %param.14) | copy-start | bytes 2752516
  59.8 4.2 %copy-start.10 = (bf16[1,3584,128]{2,1,0:T(8,128)(2,1)S(1)}, bf16[1,3584,128]{2,1,0:T(8,128)(2,1)}, u32[]{:S(2)}) copy-start(bf16[1,3584,128]{2,1,0:T(8,128)(2,1)} %param.12) | copy-start | bytes 2752516
  63.6 5.9 %collective-permute-start.1 = (bf16[256,128]{1,0:T(8,128)(2,1)S(1)}, bf16[256,128]{1,0:T(8,128)(2,1)S(1)}, u32[]{:S(2)}, u32[]{:S(2)}) collective-permute-start(bf16[256,128]{1,0:T(8,128)(2,1)S(1)} %bitcast.123), channel_id=1, source_target_pairs={{0,1},{1,0},{2,3},{3,2},{4,5},{5,4},{6,7},{7,6},{8,9},{9,8},{10,11... | collective-permute-start | bytes 196616 | tf_op jit(solution)/shard_map/ppermute | solution.py:335
  64.0 7.6 %copy-start.3 = (f32[2,2,64,3584]{3,2,1,0:T(8,128)}, f32[2,2,64,3584]{3,2,1,0:T(8,128)S(1)}, u32[]{:S(2)}) copy-start(f32[2,2,64,3584]{3,2,1,0:T(8,128)S(1)} %fusion.27) | copy-start | bytes 11010052
  64.0 5.4 %copy-start.2 = (bf16[1,2,2,64,3584]{4,3,2,1,0:T(8,128)(2,1)S(1)}, bf16[1,2,2,64,3584]{4,3,2,1,0:T(8,128)(2,1)}, u32[]{:S(2)}) copy-start(bf16[1,2,2,64,3584]{4,3,2,1,0:T(8,128)(2,1)} %param.9) | copy-start | bytes 5505028
  74.7 9.3 %collective-permute-start.3 = (bf16[256,3584]{1,0:T(8,128)(2,1)}, bf16[256,3584]{1,0:T(8,128)(2,1)}, u32[]{:S(2)}, u32[]{:S(2)}) collective-permute-start(bf16[256,3584]{1,0:T(8,128)(2,1)} %fusion.15), channel_id=1, source_target_pairs={{128,0},{129,1},{130,2},{131,3},{132,4},{133,5},{134,6},{135,7},{1... | collective-permute-start | bytes 5505032 | tf_op jit(solution)/shard_map/ppermute | solution.py:357
  76.7 1.3 copy-start.7
  87.2 1.2 copy-start.4
  96.5 4.3 %copy-start.5 = (bf16[256,3584]{1,0:T(8,128)(2,1)S(1)}, bf16[256,3584]{1,0:T(8,128)(2,1)}, u32[]{:S(2)}) copy-start(bf16[256,3584]{1,0:T(8,128)(2,1)} %copy-done.4) | copy-start | bytes 5505028
  96.5 4.3 %copy-start.12 = (bf16[4,64,7,128]{3,2,1,0:T(8,128)(2,1)S(1)}, bf16[4,64,7,128]{3,2,1,0:T(8,128)(2,1)}, u32[]{:S(2)}) copy-start(bf16[4,64,7,128]{3,2,1,0:T(8,128)(2,1)} %copy.21) | copy-start | bytes 1376260
  98.7 7.6 %collective-permute-start.4 = (bf16[256,128]{1,0:T(8,128)(2,1)S(1)}, bf16[256,128]{1,0:T(8,128)(2,1)S(1)}, u32[]{:S(2)}, u32[]{:S(2)}) collective-permute-start(bf16[256,128]{1,0:T(8,128)(2,1)S(1)} %bitcast.121), channel_id=1, source_target_pairs={{0,1},{1,0},{2,3},{3,2},{4,5},{5,4},{6,7},{7,6},{8,9},{9,8},{10,11... | collective-permute-start | bytes 196616 | tf_op jit(solution)/shard_map/ppermute | solution.py:335
  100.8 4.8 %copy-start.8 = (bf16[1,2,2,64,3584]{4,3,2,1,0:T(8,128)(2,1)S(1)}, bf16[1,2,2,64,3584]{4,3,2,1,0:T(8,128)(2,1)}, u32[]{:S(2)}) copy-start(bf16[1,2,2,64,3584]{4,3,2,1,0:T(8,128)(2,1)} %copy-done.7) | copy-start | bytes 5505028
  110.9 2.8 %copy-start.1 = (bf16[3584,896]{1,0:T(8,128)(2,1)S(1)}, bf16[3584,896]{1,0:T(8,128)(2,1)}, u32[]{:S(2)}) copy-start(bf16[3584,896]{1,0:T(8,128)(2,1)} %convolution_convert_fusion) | copy-start | bytes 19267588
  113.7 57.8 %copy-start.6 = (bf16[256,3584]{1,0:T(8,128)(2,1)S(1)}, bf16[256,3584]{1,0:T(8,128)(2,1)}, u32[]{:S(2)}) copy-start(bf16[256,3584]{1,0:T(8,128)(2,1)} %copy-done.4) | copy-start | bytes 5505028
  113.7 57.8 %copy-start.9 = (f32[256,3584]{1,0:T(8,128)S(1)}, f32[256,3584]{1,0:T(8,128)}, u32[]{:S(2)}) copy-start(f32[256,3584]{1,0:T(8,128)} %get-tuple-element.20) | copy-start | bytes 11010052

commit v2 on v1

v2 whole, which is shorter than its diff:
```python
import functools

import jax
import jax.numpy as jnp
from jax import lax
from jax.experimental import pallas as pl
from jax.experimental.pallas import tpu as pltpu
from jax.sharding import PartitionSpec as P

HEAD_DIM = 128
EPSILON = 1e-06
DPO_BETA = 0.25
LIKELIHOOD_COEF = 0.2
MESH = pl.DeviceIdType.MESH
BF = jnp.bfloat16
F32 = jnp.float32
COLS = 512


class Flow:
    def __init__(self, size, place, ahead, behind, local, landing, sends, receives, base, hops):
        self.size, self.place = size, place
        self.target = {1: ahead, -1: behind}
        self.local, self.landing = local, landing
        self.sends, self.receives = sends, receives
        self.hops = hops
        self.slot = {}
        for (way, half), count in hops.items():
            for step in range(count):
                self.slot[way, half, step] = base + len(self.slot)
        self.count = len(self.slot)
        self.copies = {}

    def copy(self, way, half, step):
        slot = self.slot[way, half, step]
        chunk = lax.rem(self.place + way * (self.hops[way, half] - step) + self.size, self.size)
        return chunk, pltpu.make_async_remote_copy(
            src_ref=self.local(chunk, half),
            dst_ref=self.landing(slot),
            send_sem=self.sends.at[slot],
            recv_sem=self.receives.at[slot],
            device_id=self.target[way],
            device_id_type=MESH,
        )

    def collect(self, way, half, step, chunk):
        self.copies[way, half, step].wait_recv()
        target = self.local(chunk, half)
        landed = self.landing(self.slot[way, half, step])
        add_into(target, landed)

    def step(self, step):
        for way, half in self.hops:
            if step < self.hops[way, half]:
                chunk, copy = self.copy(way, half, step)
                if step:
                    self.collect(way, half, step - 1, chunk)
                copy.start()
                self.copies[way, half, step] = copy

    def finish(self):
        for (way, half), count in self.hops.items():
            self.collect(way, half, count - 1, self.place)

    def drain(self):
        for copy in self.copies.values():
            copy.wait_send()


def add_into(target, landed):
    if len(target.shape) > 2 and target.shape[-2] > 1:

        def one(index, carry):
            target[index] = target[index] + landed[index]
            return carry

        lax.fori_loop(0, target.shape[0], one, 0)
    else:
        target[...] = target[...] + landed[...]


class Spread:
    def __init__(self, size, place, ahead, behind, own, landing, sends, receives, base):
        self.own, self.landing = own, landing
        self.sends, self.receives = sends, receives
        self.target = {1: ahead, -1: behind}
        self.hops = {1: size // 2, -1: size - 1 - size // 2}
        self.base = base
        self.count = size - 1
        self.copies = {}

    def slot(self, way, step):
        return step if way == 1 else self.hops[1] + step

    def step(self, step):
        for way, count in self.hops.items():
            if step < count:
                if step:
                    self.copies[way, step - 1].wait_recv()
                slot = self.slot(way, step)
                source = self.landing.at[self.slot(way, step - 1)] if step else self.own
                copy = pltpu.make_async_remote_copy(
                    src_ref=source,
                    dst_ref=self.landing.at[slot],
                    send_sem=self.sends.at[self.base + slot],
                    recv_sem=self.receives.at[self.base + slot],
                    device_id=self.target[way],
                    device_id_type=MESH,
                )
                copy.start()
                self.copies[way, step] = copy

    def finish(self):
        for way, count in self.hops.items():
            if count:
                self.copies[way, count - 1].wait_recv()
        total = self.own[...]
        for slot in range(self.count):
            total = total + self.landing[slot]
        return total

    def drain(self):
        for copy in self.copies.values():
            copy.wait_send()


WIDTH = 3584
TOKENS = 256
BLOCK = 256
BLOCKS = WIDTH // BLOCK
LENGTH = 64
HEADS = 7


def wide(rows):
    return jnp.concatenate([rows, rows], axis=1)


def step_kernel(
    bounds,
    reference,
    logprob,
    gain,
    inputs_hbm,
    pattern_hbm,
    value_hbm,
    output_hbm,
    head_hbm,
    mixed_out,
    value_out,
    gain_out,
    cotangent_out,
    inputs,
    pattern,
    weight,
    weight_other,
    weight_out,
    head_own,
    head_other,
    upstream,
    below,
    normed,
    values,
    mixed,
    mixed_grad,
    grad,
    grad_other,
    normed_grad,
    rms,
    gain_row,
    counts,
    land_cz,
    land_cy,
    land_cx,
    part_a,
    part_b,
    part_g,
    land_a1,
    land_b1,
    land_a2,
    land_b2,
    land_g1,
    land_g2,
    last_src,
    last_dst,
    last_g,
    load_sems,
    pass_sends,
    pass_receives,
    go,
    sends,
    receives,
):
    pipe = lax.axis_index("pipe")
    tensor = lax.axis_index("tensor")
    dp = lax.axis_index("dp")
    z = dp // 8
    y = lax.rem(dp, 8) // 2
    x = lax.rem(dp, 2)

    def device(z_at, y_at, x_at):
        return (pipe, z_at * 8 + y_at * 2 + x_at, tensor)

    z_next, z_prev = lax.rem(z + 1, 8), lax.rem(z + 7, 8)
    y_next, y_prev = lax.rem(y + 1, 4), lax.rem(y + 3, 4)
    z_ways = (device(z_next, y, x), device(z_prev, y, x))
    y_ways = (device(z, y_next, x), device(z, y_prev, x))
    x_way = device(z, y, 1 - x)
    peer = (pipe, dp, 1 - tensor)
    cross = (pipe, z * 8 + y * 2 + 1 - x, 1 - tensor)
    partner = (1 - pipe, dp, tensor)

    loads = {
        name: pltpu.make_async_copy(source, target, load_sems.at[index])
        for index, (name, source, target) in enumerate(
            (
                ("inputs", inputs_hbm, inputs),
                ("weight", value_hbm, weight),
                ("pattern", pattern_hbm, pattern),
                ("head", head_hbm, head_own),
                ("output", output_hbm, weight_out),
            )
        )
    }
    for load in loads.values():
        load.start()

    def token_rows(pair, which):
        lanes = lax.broadcasted_iota(jnp.int32, (1, LENGTH), 1)
        rows = lax.broadcasted_iota(jnp.int32, (LENGTH, 1), 0)
        first, end = bounds[pair, 0], bounds[pair, 1 + which]
        row_mask = ((lanes >= first) & (lanes < end)).astype(F32)
        column_mask = ((rows >= first) & (rows < end)).astype(F32)
        return row_mask, column_mask

    own_count = jnp.zeros((1, 1), F32)
    for pair in range(2):
        own_count = own_count + jnp.sum(token_rows(pair, 0)[0], axis=1, keepdims=True)
    counts[0] = jnp.broadcast_to(own_count, (1, 128))
    part_g[...] = jnp.zeros_like(part_g)

    barrier = pltpu.get_barrier_semaphore()
    for neighbour in (*z_ways, *y_ways, x_way, peer, cross, partner):
        pl.semaphore_signal(barrier, inc=1, device_id=neighbour, device_id_type=MESH)
    pl.semaphore_wait(barrier, 8)

    def passing(index, source, target, to):
        return pltpu.make_async_remote_copy(
            src_ref=source,
            dst_ref=target,
            send_sem=pass_sends.at[index],
            recv_sem=pass_receives.at[index],
            device_id=to,
            device_id_type=MESH,
        )

    send_head = passing(0, head_hbm, head_other, peer)
    send_weight = passing(1, value_hbm, weight_other, cross)
    send_grad = passing(2, grad, grad_other, peer)
    send_below = [
        passing(3 + pair, below.at[pl.ds(128 * pair, 128)], upstream.at[pl.ds(128 * pair, 128)], partner)
        for pair in range(2)
    ]

    @pl.when(pipe == 1)
    def _():
        send_head.start()

    base = 0

    def spread(size, place, ways, own, landing):
        nonlocal base
        made = Spread(size, place, *ways, own, landing, sends, receives, base)
        base += made.count
        return made

    count_z = spread(8, z, z_ways, counts.at[0], land_cz)
    count_y = spread(4, y, y_ways, counts.at[1], land_cy)
    count_x = spread(2, x, (x_way, x_way), counts.at[2], land_cx)

    count_z.step(0)
    loads["inputs"].wait()

    def square(index, total):
        at = pl.ds(pl.multiple_of(index * BLOCK, BLOCK), BLOCK)
        block = inputs[:, at].astype(F32)
        block = block * block
        return total + block[:, :128] + block[:, 128:]

    total = lax.fori_loop(0, BLOCKS, square, jnp.zeros((TOKENS, 128), F32))
    mean = jnp.sum(total, axis=1, keepdims=True) / WIDTH
    rms[...] = jnp.broadcast_to(lax.rsqrt(mean + EPSILON), (TOKENS, 128))
    count_z.step(1)
    loads["weight"].wait()

    def project(index, total):
        at = pl.ds(pl.multiple_of(index * BLOCK, BLOCK), BLOCK)
        block = (inputs[:, at].astype(F32) * wide(rms[...]) * gain[:, at]).astype(BF)
        normed[:, at] = block
        return total + jnp.dot(block, weight[at, :], preferred_element_type=F32)

    total = lax.fori_loop(0, BLOCKS // 2, project, jnp.zeros((TOKENS, 128), F32))
    count_z.step(2)
    total = lax.fori_loop(BLOCKS // 2, BLOCKS, project, total)
    values[...] = total.astype(BF)
    count_z.step(3)
    loads["pattern"].wait()

    def mix(index, carry):
        rows = pl.ds(pl.multiple_of(index * LENGTH, LENGTH), LENGTH)
        block = jnp.dot(pattern[index], values[rows, :], preferred_element_type=F32).astype(BF)
        for head in range(HEADS):
            mixed[rows, head * 128 : (head + 1) * 128] = block[head * LENGTH : (head + 1) * LENGTH]
        return carry

    lax.fori_loop(0, 2, mix, 0)
    counts[1] = count_z.finish()
    lax.fori_loop(2, 4, mix, 0)
    count_y.step(0)
    count_y.step(1)
    counts[2] = count_y.finish()
    loads["head"].wait()
    count_x.step(0)
    total_count = count_x.finish()[:, :1]
    loads["output"].wait()

    @pl.when(pipe == 1)
    def _():
        scale = jnp.full((1, 1), LIKELIHOOD_COEF * 128, F32) / total_count
        for pair in range(2):
            masks = [token_rows(pair, which) for which in range(2)]
            sums = [
                jnp.sum(masks[which][0] * logprob[pair, which : which + 1, :], axis=1, keepdims=True)
                for which in range(2)
            ]
            margin = DPO_BETA * (
                sums[0] - reference[pair, 0] - (sums[1] - reference[pair, 1])
            )
            pair_weight = jax.nn.sigmoid(-margin)
            chosen = -DPO_BETA * pair_weight * masks[0][1] - scale * masks[0][1]
            rejected = DPO_BETA * pair_weight * masks[1][1]
            mine = jnp.where(tensor == 0, chosen, rejected)
            theirs = jnp.where(tensor == 0, rejected, chosen)
            rows = pl.ds(pl.multiple_of((2 * pair + tensor) * LENGTH, LENGTH), LENGTH)
            upstream[rows, :] = (mine * head_own[pair].astype(F32)).astype(BF)
            if pair == 0:
                kept = theirs
        send_head.wait_recv()
        for pair, theirs in enumerate((kept, theirs)):
            rows = pl.ds(pl.multiple_of((2 * pair + 1 - tensor) * LENGTH, LENGTH), LENGTH)
            upstream[rows, :] = (theirs * head_other[pair].astype(F32)).astype(BF)
        send_weight.start()

    @pl.when(pipe == 0)
    def _():
        pl.semaphore_wait(go, 1)
        send_weight.start()
        for send in send_below:
            send.wait_recv()

    def heads_back(first, count):
        rows = pl.ds(pl.multiple_of(first * 128, 128), count * 128)
        block = lax.dot_general(
            upstream[...], weight_out[rows, :], (((1,), (1,)), ((), ())), preferred_element_type=F32
        ).astype(BF)
        for head in range(count):
            at = pl.ds(pl.multiple_of((first + head) * LENGTH, LENGTH), LENGTH)
            for index in range(4):
                mixed_grad[index, at, :] = block[
                    index * LENGTH : (index + 1) * LENGTH, head * 128 : (head + 1) * 128
                ]

    def two_heads(index, carry):
        heads_back(2 * index, 2)
        return carry

    lax.fori_loop(0, 3, two_heads, 0)
    heads_back(6, 1)

    @pl.when(pipe == 1)
    def _():
        pl.semaphore_signal(go, inc=1, device_id=partner, device_id_type=MESH)

    def unmix(index, carry):
        rows = pl.ds(pl.multiple_of(index * LENGTH, LENGTH), LENGTH)
        grad[rows, :] = lax.dot_general(
            pattern[index], mixed_grad[index], (((0,), (0,)), ((), ())), preferred_element_type=F32
        ).astype(BF)
        return carry

    lax.fori_loop(0, 4, unmix, 0)
    send_grad.start()

    def products(index, carry):
        at = pl.ds(pl.multiple_of(index * 896, 128), 896)
        places = pl.ds(2 * index, 2)
        turned = upstream[:, at].T
        block = jnp.dot(turned, mixed[:, :COLS], preferred_element_type=F32).astype(BF)
        part_a[places] = block.reshape(2, 4, 112, COLS)
        block = jnp.dot(turned, mixed[:, COLS:], preferred_element_type=F32).astype(BF)
        part_b[places, :, :, : COLS - HEAD_DIM] = block.reshape(2, 4, 112, COLS - HEAD_DIM)
        block = jnp.dot(normed[:, at].T, grad[...], preferred_element_type=F32).astype(BF)
        part_b[places, :, :, COLS - HEAD_DIM :] = block.reshape(2, 4, 112, HEAD_DIM)
        return carry

    lax.fori_loop(0, 4, products, 0)

    def flow(size, place, ways, local, landing, hops):
        nonlocal base
        first = base
        made = Flow(
            size, place, *ways, local, lambda slot: landing.at[slot - first], sends, receives, base, hops
        )
        base += made.count
        return made

    z_halves = {(1, 0): 4, (-1, 1): 4, (1, 1): 3, (-1, 0): 3}
    y_halves = {(1, 0): 2, (-1, 1): 2, (1, 1): 1, (-1, 0): 1}
    z_whole = {(1, 0): 4, (-1, 0): 3}
    y_whole = {(1, 0): 2, (-1, 0): 1}
    a1 = flow(8, z, z_ways, lambda q, h: part_a.at[q, pl.ds(2 * h, 2)], land_a1, z_halves)
    b1 = flow(4, y, y_ways, lambda q, h: part_b.at[pl.ds(4 * h, 4), q], land_b1, y_halves)
    a2 = flow(4, y, y_ways, lambda q, h: part_a.at[z, q], land_a2, y_whole)
    b2 = flow(8, z, z_ways, lambda q, h: part_b.at[q, y], land_b2, z_whole)
    g1 = flow(8, z, z_ways, lambda q, h: part_g.at[q], land_g1, z_whole)
    g2 = flow(4, y, y_ways, lambda q, h: part_g.at[z, q], land_g2, y_whole)

    a1.step(0)
    b1.step(0)
    send_weight.wait_recv()
    send_grad.wait_recv()

    def norm_back(index, total):
        at = pl.ds(pl.multiple_of(index * BLOCK, BLOCK), BLOCK)
        last_dims = (((1,), (1,)), ((), ()))
        mine = lax.dot_general(grad[...], weight[at, :], last_dims, preferred_element_type=F32)
        theirs = lax.dot_general(
            grad_other[...], weight_other[at, :], last_dims, preferred_element_type=F32
        )
        both = mine.astype(BF).astype(F32) + theirs.astype(BF).astype(F32)
        normed_grad[:, at] = both
        term = both * inputs[:, at].astype(F32)
        gain_row[:, at] = jnp.sum(term * wide(rms[...]), axis=0, keepdims=True)
        term = term * gain[:, at]
        return total + term[:, :128] + term[:, 128:]

    total = lax.fori_loop(0, BLOCKS, norm_back, jnp.zeros((TOKENS, 128), F32))
    mean = jnp.sum(total, axis=1, keepdims=True) / WIDTH
    cubed = rms[...] * rms[...] * rms[...] * mean
    normed_grad_scale = cubed
    outputs = []
    for pair in range(2):
        rows = pl.ds(128 * pair, 128)
        slope = wide(normed_grad_scale[128 * pair : 128 * (pair + 1)])

        def through(index, carry):
            at = pl.ds(pl.multiple_of(index * BLOCK, BLOCK), BLOCK)
            scaled = normed_grad[rows, at] * gain[:, at]
            change = wide(rms[rows, :]) * scaled - inputs[rows, at].astype(F32) * slope
            below[rows, at] = (upstream[rows, at].astype(F32) + change).astype(BF)
            return carry

        lax.fori_loop(0, BLOCKS, through, 0)

        @pl.when(pipe == 1)
        def _():
            send_below[pair].start()

        own = pl.ds(pl.multiple_of((2 * pair + tensor) * LENGTH, LENGTH), LENGTH)
        output = pltpu.make_async_copy(below.at[own], cotangent_out.at[pair], load_sems.at[5 + pair])
        output.start()
        outputs.append(output)

    for place in range(32):
        part_g[place // 4, place % 4, :, :112] = gain_row[:, 112 * place : 112 * (place + 1)]

    def last(index, source, target):
        return pltpu.make_async_remote_copy(
            src_ref=source,
            dst_ref=target,
            send_sem=sends.at[base + index],
            recv_sem=receives.at[base + index],
            device_id=x_way,
            device_id_type=MESH,
        )

    def exchange(index, part):
        total = part[z, y].astype(F32)
        low, high = total[:56], total[56:]
        last_src[index] = jnp.where(x == 0, high, low).astype(BF)
        copy = last(index, last_src.at[index], last_dst.at[index])
        copy.start()
        return copy, jnp.where(x == 0, low, high)

    a1.step(1)
    g1.step(0)
    b1.step(1)
    g1.step(1)
    a1.step(2)
    g1.step(2)
    a1.step(3)
    g1.step(3)
    b1.finish()
    b2.step(0)
    a1.finish()
    a2.step(0)
    g1.finish()
    g2.step(0)
    b2.step(1)
    a2.step(1)
    g2.step(1)
    b2.step(2)
    a2.finish()
    copy_a, own_a = exchange(0, part_a)
    mixed_out[:, :COLS] = own_a
    g2.finish()
    copy_g = last(2, part_g.at[z, y], last_g)
    copy_g.start()
    b2.step(3)
    b2.finish()
    copy_b, own_b = exchange(1, part_b)
    mixed_out[:, COLS:] = own_b[:, : COLS - HEAD_DIM]
    value_out[...] = own_b[:, COLS - HEAD_DIM :]
    copy_a.wait_recv()
    mixed_out[:, :COLS] += last_dst[0].astype(F32)
    copy_g.wait_recv()
    gain_total = part_g[z, y] + last_g[...]
    gain_out[...] = jnp.where(x == 0, gain_total[:, :56], gain_total[:, 56:112])
    copy_b.wait_recv()
    landed = last_dst[1].astype(F32)
    mixed_out[:, COLS:] += landed[:, : COLS - HEAD_DIM]
    value_out[...] += landed[:, COLS - HEAD_DIM :]
    for made in (count_z, count_y, count_x, a1, b1, a2, b2, g1, g2):
        made.drain()
    for copy in (copy_a, copy_b, copy_g, send_weight, send_grad):
        copy.wait_send()
    for output in outputs:
        output.wait()

    @pl.when(pipe == 1)
    def _():
        send_head.wait_send()
        for send in send_below:
            send.wait_send()


def body(
    hidden_in,
    attention_probs,
    norm_gain,
    value_weight,
    output_weight,
    head_grad,
    policy_logprob,
    reference_logprob,
    sequence_bounds,
):
    copies = 7 + 3 + 1 + 14 + 6 + 3 + 7 + 7 + 3 + 3
    vmem = pl.BlockSpec(memory_space=pltpu.VMEM)
    smem = pl.BlockSpec(memory_space=pltpu.SMEM)
    hbm = pl.BlockSpec(memory_space=pl.ANY)
    mixed_share, value_share, gain_share, own_output = pl.pallas_call(
        step_kernel,
        out_shape=(
            jax.ShapeDtypeStruct((56, HEADS * HEAD_DIM), F32),
            jax.ShapeDtypeStruct((56, HEAD_DIM), F32),
            jax.ShapeDtypeStruct((1, 56), F32),
            jax.ShapeDtypeStruct((2, LENGTH, WIDTH), BF),
        ),
        in_specs=[smem, smem, vmem, vmem, hbm, hbm, hbm, hbm, hbm],
        out_specs=(vmem, vmem, vmem, hbm),
        scratch_shapes=[
            pltpu.VMEM((TOKENS, WIDTH), BF),
            pltpu.VMEM((4, HEADS * LENGTH, LENGTH), BF),
            pltpu.VMEM((WIDTH, HEAD_DIM), BF),
            pltpu.VMEM((WIDTH, HEAD_DIM), BF),
            pltpu.VMEM((HEADS * HEAD_DIM, WIDTH), BF),
            pltpu.VMEM((2, LENGTH, WIDTH), BF),
            pltpu.VMEM((2, LENGTH, WIDTH), BF),
            pltpu.VMEM((TOKENS, WIDTH), BF),
            pltpu.VMEM((TOKENS, WIDTH), BF),
            pltpu.VMEM((TOKENS, WIDTH), BF),
            pltpu.VMEM((TOKENS, HEAD_DIM), BF),
            pltpu.VMEM((TOKENS, HEADS * HEAD_DIM), BF),
            pltpu.VMEM((4, HEADS * LENGTH, HEAD_DIM), BF),
            pltpu.VMEM((TOKENS, HEAD_DIM), BF),
            pltpu.VMEM((TOKENS, HEAD_DIM), BF),
            pltpu.VMEM((TOKENS, WIDTH), F32),
            pltpu.VMEM((TOKENS, 128), F32),
            pltpu.VMEM((1, WIDTH), F32),
            pltpu.VMEM((3, 1, 128), F32),
            pltpu.VMEM((7, 1, 128), F32),
            pltpu.VMEM((3, 1, 128), F32),
            pltpu.VMEM((1, 1, 128), F32),
            pltpu.VMEM((8, 4, 112, COLS), BF),
            pltpu.VMEM((8, 4, 112, COLS), BF),
            pltpu.VMEM((8, 4, 1, 128), F32),
            pltpu.VMEM((14, 2, 112, COLS), BF),
            pltpu.VMEM((6, 4, 112, COLS), BF),
            pltpu.VMEM((3, 112, COLS), BF),
            pltpu.VMEM((7, 112, COLS), BF),
            pltpu.VMEM((7, 4, 1, 128), F32),
            pltpu.VMEM((3, 1, 128), F32),
            pltpu.VMEM((2, 56, COLS), BF),
            pltpu.VMEM((2, 56, COLS), BF),
            pltpu.VMEM((1, 128), F32),
            pltpu.SemaphoreType.DMA((7,)),
            pltpu.SemaphoreType.DMA((5,)),
            pltpu.SemaphoreType.DMA((5,)),
            pltpu.SemaphoreType.REGULAR,
            pltpu.SemaphoreType.DMA((copies,)),
            pltpu.SemaphoreType.DMA((copies,)),
        ],
        compiler_params=pltpu.CompilerParams(
            collective_id=0, has_side_effects=True, vmem_limit_bytes=60 * 1024 * 1024
        ),
    )(
        sequence_bounds,
        reference_logprob,
        policy_logprob,
        norm_gain,
        hidden_in.reshape(TOKENS, WIDTH),
        attention_probs.reshape(4, HEADS * LENGTH, LENGTH),
        value_weight[0],
        output_weight[0],
        head_grad.reshape(2, LENGTH, WIDTH),
    )
    return (
        own_output.reshape(1, 2, 1, LENGTH, WIDTH),
        value_share[None],
        mixed_share[None],
        gain_share,
    )


def solution(mesh):
    in_specs = (
        P("pipe", "dp", None, None, None),
        P("pipe", "dp", None, "tensor", None, None),
        P("pipe", None),
        P("pipe", None, "tensor"),
        P("pipe", "tensor", None),
        P("dp", "tensor", None, None),
        P("dp", None, None),
        P("dp", None),
        P("dp", None),
    )
    out_specs = (
        P("pipe", "dp", "tensor", None, None),
        P("pipe", "dp", "tensor"),
        P("pipe", "dp", "tensor"),
        P("pipe", "dp"),
    )
    return jax.shard_map(body, mesh=mesh, in_specs=in_specs, out_specs=out_specs, check_vma=False)
```

time: 177 us -> 112 us (0.63)
  Pallas kernels: 57.8 us -> 105 us
  blocking collectives: 40.5 us -> 0 us
  matrix products: 28.5 us -> 0 us
  other arithmetic: 16 us -> 0 us
  local copies, waits for them, and re-layouts: 15.9 us -> 6.31 us
  waiting for transfers between devices: 8.73 us -> 0 us
  starting transfers between devices: 6.74 us -> 0 us
    pallas_call x1, Pallas kernels: 57.8 us -> 105 us  [body(): pl.pallas_call(step_kernel, out_shape=(jax.ShapeDtypeStruct((56, HEADS *...]
    psum x1 -> x0, blocking collectives: 40.5 us -> none  [body(): chosen_total = lax.psum(local_count, 'dp')]
    dot_general x12 -> x0, matrix products: 28.5 us -> none  [the longest x2 11.5 us: through(): jnp.einsum('nd,hd->nh', upstream, output_matrix, preferred_element_type=F32)]
    ppermute x5 -> x0, waiting for transfers between devices: 8.73 us -> none  [the longest x2 4.72 us: through(): other_grad = lax.ppermute(values_grad, 'tensor', [(0, 1), (1, 0)])]
    convert_element_type x6 -> x0, other arithmetic: 7.49 us -> none  [the longest x2 4.66 us: through(): below = (upstream.astype(F32) + input_grad).astype(BF)]
    ppermute x5 -> x0, starting transfers between devices: 6.74 us -> none  [the longest x2 2.21 us: through(): other_grad = lax.ppermute(values_grad, 'tensor', [(0, 1), (1, 0)])]
    reshape x3 -> x0, local copies, waits for them, and re-layouts: 4.85 us -> none  [the longest x2 4.75 us: through(): mixed_heads = mixed_grad.reshape(pairs * 2, length, heads, HEAD_DIM)]
    reduce_sum x3 -> x0, other arithmetic: 3.42 us -> none  [the longest x1 1.94 us: body(): jnp.mean(input_float * input_float, axis=-1, keepdims=True) + EPSILON]
  transfers between devices with their start and end apart: 5 -> 0, of which waited for: 2 -> 0; matrix products, arithmetic and copies ran while one was open for 16% -> 0% of each run, Pallas kernels for 0% -> 0%
where the time goes in v2:
time: 112 us
  Pallas kernels  105 us (94%)
  local copies, waits for them, and re-layouts  6.31 us (6%)
    pallas_call x1, Pallas kernels, body(): pl.pallas_call(step_kernel, out_shape=(jax.ShapeDtypeStruct((56, HEADS *...  105 us
    unnamed x4, local copies, waits for them, and re-layouts  6.31 us

profile of v2, /device:TPU:2, one launch (start us, length us, event | category | flops | bytes accessed | tf_op | source)
XLA Modules:
  0.0 111.6 jit_solution(7583131235025948058)
XLA Ops:
  0.6 104.7 %shard_map.120 = (f32[56,896]{1,0:T(8,128)}, f32[56,128]{1,0:T(8,128)}, f32[1,56]{1,0:T(1,128)}, bf16[2,64,3584]{2,1,0:T(8,128)(2,1)}) custom-call(s32[2,3]{1,0:T(2,128)} %bounds.1, f32[2,2]{1,0:T(2,128)} %reference.1, f32[2,2,64]{2,1,0:T(2,128)} %logprob.1, f32[1,3584]{1,0:T(1,128)} %gain.1, bf16[256,3584]{1,0:T(8,128)(2,1)} %bitcast.11, ...), custom_call_target="tpu_custom_call" | custom-call | tf_op jit(solution)/shard_map/pallas_call | solution.py:562
  105.3 2.2 %copy.18 = bf16[1,2,1,64,3584]{4,3,2,1,0:T(8,128)(2,1)} copy(bf16[1,2,1,64,3584]{4,3,2,1,0:T(8,128)(2,1)} %bitcast.14) | data formatting | bytes 1835008
  107.5 1.4 %copy.19 = f32[1,56,128]{2,1,0:T(8,128)} copy(f32[1,56,128]{2,1,0:T(8,128)} %bitcast.17) | data formatting | bytes 57344
  108.8 1.6 %copy.20 = f32[1,56,896]{2,1,0:T(8,128)} copy(f32[1,56,896]{2,1,0:T(8,128)} %bitcast.16) | data formatting | bytes 401408
  110.5 1.2 %copy.21 = f32[1,56]{1,0:T(1,128)} copy(f32[1,56]{1,0:T(1,128)} %get-tuple-element.23) | data formatting | bytes 448

commit v3 on v2

--- a/solution.py
+++ b/solution.py
@@ -15,6 +15,7 @@
 BF = jnp.bfloat16
 F32 = jnp.float32
 COLS = 512
+SPLIT = 384
 
 
 class Flow:
@@ -34,20 +35,26 @@
     def copy(self, way, half, step):
         slot = self.slot[way, half, step]
         chunk = lax.rem(self.place + way * (self.hops[way, half] - step) + self.size, self.size)
+        source = self.local(chunk, half)
         return chunk, pltpu.make_async_remote_copy(
-            src_ref=self.local(chunk, half),
-            dst_ref=self.landing(slot),
+            src_ref=source,
+            dst_ref=self.landed(slot, source),
             send_sem=self.sends.at[slot],
             recv_sem=self.receives.at[slot],
             device_id=self.target[way],
             device_id_type=MESH,
         )
 
+    def landed(self, slot, like):
+        landing = self.landing(slot)
+        if landing.shape == like.shape:
+            return landing
+        return landing.at[pl.ds(0, like.shape[0])]
+
     def collect(self, way, half, step, chunk):
         self.copies[way, half, step].wait_recv()
         target = self.local(chunk, half)
-        landed = self.landing(self.slot[way, half, step])
-        add_into(target, landed)
+        add_into(target, self.landed(self.slot[way, half, step], target))
 
     def step(self, step):
         for way, half in self.hops:
@@ -80,47 +87,34 @@
 
 
 class Spread:
-    def __init__(self, size, place, ahead, behind, own, landing, sends, receives, base):
+    def __init__(self, size, place, device_at, own, landing, sends, receives, base):
         self.own, self.landing = own, landing
-        self.sends, self.receives = sends, receives
-        self.target = {1: ahead, -1: behind}
-        self.hops = {1: size // 2, -1: size - 1 - size // 2}
-        self.base = base
         self.count = size - 1
-        self.copies = {}
-
-    def slot(self, way, step):
-        return step if way == 1 else self.hops[1] + step
-
-    def step(self, step):
-        for way, count in self.hops.items():
-            if step < count:
-                if step:
-                    self.copies[way, step - 1].wait_recv()
-                slot = self.slot(way, step)
-                source = self.landing.at[self.slot(way, step - 1)] if step else self.own
-                copy = pltpu.make_async_remote_copy(
-                    src_ref=source,
-                    dst_ref=self.landing.at[slot],
-                    send_sem=self.sends.at[self.base + slot],
-                    recv_sem=self.receives.at[self.base + slot],
-                    device_id=self.target[way],
-                    device_id_type=MESH,
-                )
-                copy.start()
-                self.copies[way, step] = copy
+        self.copies = [
+            pltpu.make_async_remote_copy(
+                src_ref=own,
+                dst_ref=landing.at[slot],
+                send_sem=sends.at[base + slot],
+                recv_sem=receives.at[base + slot],
+                device_id=device_at(lax.rem(place + 1 + slot, size)),
+                device_id_type=MESH,
+            )
+            for slot in range(self.count)
+        ]
+
+    def start(self):
+        for copy in self.copies:
+            copy.start()
 
     def finish(self):
-        for way, count in self.hops.items():
-            if count:
-                self.copies[way, count - 1].wait_recv()
         total = self.own[...]
-        for slot in range(self.count):
+        for slot, copy in enumerate(self.copies):
+            copy.wait_recv()
             total = total + self.landing[slot]
         return total
 
     def drain(self):
-        for copy in self.copies.values():
+        for copy in self.copies:
             copy.wait_send()
 
 
@@ -158,6 +152,7 @@
     head_own,
     head_other,
     upstream,
+    upstream_turned,
     below,
     normed,
     values,
@@ -240,9 +235,11 @@
     part_g[...] = jnp.zeros_like(part_g)
 
     barrier = pltpu.get_barrier_semaphore()
-    for neighbour in (*z_ways, *y_ways, x_way, peer, cross, partner):
+    z_others = [device(lax.rem(z + step, 8), y, x) for step in range(1, 8)]
+    y_others = [device(z, lax.rem(y + step, 4), x) for step in range(1, 4)]
+    for neighbour in (*z_others, *y_others, x_way, peer, cross, partner):
         pl.semaphore_signal(barrier, inc=1, device_id=neighbour, device_id_type=MESH)
-    pl.semaphore_wait(barrier, 8)
+    pl.semaphore_wait(barrier, 14)
 
     def passing(index, source, target, to):
         return pltpu.make_async_remote_copy(
@@ -268,17 +265,17 @@
 
     base = 0
 
-    def spread(size, place, ways, own, landing):
+    def spread(size, place, device_at, own, landing):
         nonlocal base
-        made = Spread(size, place, *ways, own, landing, sends, receives, base)
+        made = Spread(size, place, device_at, own, landing, sends, receives, base)
         base += made.count
         return made
 
-    count_z = spread(8, z, z_ways, counts.at[0], land_cz)
-    count_y = spread(4, y, y_ways, counts.at[1], land_cy)
-    count_x = spread(2, x, (x_way, x_way), counts.at[2], land_cx)
-
-    count_z.step(0)
+    count_z = spread(8, z, lambda at: device(at, y, x), counts.at[0], land_cz)
+    count_y = spread(4, y, lambda at: device(z, at, x), counts.at[1], land_cy)
+    count_x = spread(2, x, lambda at: device(z, y, at), counts.at[2], land_cx)
+
+    count_z.start()
     loads["inputs"].wait()
 
     def square(index, total):
@@ -290,7 +287,6 @@
     total = lax.fori_loop(0, BLOCKS, square, jnp.zeros((TOKENS, 128), F32))
     mean = jnp.sum(total, axis=1, keepdims=True) / WIDTH
     rms[...] = jnp.broadcast_to(lax.rsqrt(mean + EPSILON), (TOKENS, 128))
-    count_z.step(1)
     loads["weight"].wait()
 
     def project(index, total):
@@ -299,11 +295,10 @@
         normed[:, at] = block
         return total + jnp.dot(block, weight[at, :], preferred_element_type=F32)
 
-    total = lax.fori_loop(0, BLOCKS // 2, project, jnp.zeros((TOKENS, 128), F32))
-    count_z.step(2)
-    total = lax.fori_loop(BLOCKS // 2, BLOCKS, project, total)
+    total = lax.fori_loop(0, BLOCKS, project, jnp.zeros((TOKENS, 128), F32))
     values[...] = total.astype(BF)
-    count_z.step(3)
+    counts[1] = count_z.finish()
+    count_y.start()
     loads["pattern"].wait()
 
     def mix(index, carry):
@@ -314,13 +309,10 @@
         return carry
 
     lax.fori_loop(0, 2, mix, 0)
-    counts[1] = count_z.finish()
+    counts[2] = count_y.finish()
+    count_x.start()
     lax.fori_loop(2, 4, mix, 0)
-    count_y.step(0)
-    count_y.step(1)
-    counts[2] = count_y.finish()
     loads["head"].wait()
-    count_x.step(0)
     total_count = count_x.finish()[:, :1]
     loads["output"].wait()
 
@@ -346,10 +338,10 @@
             if pair == 0:
                 kept = theirs
         send_head.wait_recv()
+        send_weight.start()
         for pair, theirs in enumerate((kept, theirs)):
             rows = pl.ds(pl.multiple_of((2 * pair + 1 - tensor) * LENGTH, LENGTH), LENGTH)
             upstream[rows, :] = (theirs * head_other[pair].astype(F32)).astype(BF)
-        send_weight.start()
 
     @pl.when(pipe == 0)
     def _():
@@ -357,6 +349,39 @@
         send_weight.start()
         for send in send_below:
             send.wait_recv()
+
+    def flow(size, place, ways, local, landing, hops):
+        nonlocal base
+        first = base
+        made = Flow(
+            size, place, *ways, local, lambda slot: landing.at[slot - first], sends, receives, base, hops
+        )
+        base += made.count
+        return made
+
+    z_halves = {(1, 0): 4, (-1, 1): 4, (1, 1): 3, (-1, 0): 3}
+    y_halves = {(1, 0): 2, (-1, 1): 2, (1, 1): 1, (-1, 0): 1}
+    z_whole = {(1, 0): 4, (-1, 0): 3}
+    y_whole = {(1, 0): 2, (-1, 0): 1}
+    rows_of = (pl.ds(0, 64), pl.ds(64, 48))
+    a1 = flow(8, z, z_ways, lambda q, h: part_a.at[q, pl.ds(2 * h, 2)], land_a1, z_halves)
+    b1 = flow(4, y, y_ways, lambda q, h: part_b.at[pl.ds(4 * h, 4), q], land_b1, y_halves)
+    a2 = flow(4, y, y_ways, lambda q, h: part_a.at[z, q, rows_of[h]], land_a2, y_halves)
+    b2 = flow(8, z, z_ways, lambda q, h: part_b.at[q, y, rows_of[h]], land_b2, z_halves)
+    g1 = flow(8, z, z_ways, lambda q, h: part_g.at[q], land_g1, z_whole)
+    g2 = flow(4, y, y_ways, lambda q, h: part_g.at[z, q], land_g2, y_whole)
+
+    def later_products(index, carry):
+        at = pl.ds(pl.multiple_of(index * 896, 128), 896)
+        rows = pl.ds(pl.multiple_of(index * 896, 128), 896)
+        places = pl.ds(2 * index, 2)
+        upstream_turned[rows, :] = upstream[:, at].T
+        block = jnp.dot(upstream_turned[rows, :], mixed[:, SPLIT:], preferred_element_type=F32)
+        part_b[places] = block.astype(BF).reshape(2, 4, 112, COLS)
+        return carry
+
+    lax.fori_loop(0, 4, later_products, 0)
+    b1.step(0)
 
     def heads_back(first, count):
         rows = pl.ds(pl.multiple_of(first * 128, 128), count * 128)
@@ -391,67 +416,46 @@
     lax.fori_loop(0, 4, unmix, 0)
     send_grad.start()
 
-    def products(index, carry):
+    def first_products(index, carry):
         at = pl.ds(pl.multiple_of(index * 896, 128), 896)
+        rows = pl.ds(pl.multiple_of(index * 896, 128), 896)
         places = pl.ds(2 * index, 2)
-        turned = upstream[:, at].T
-        block = jnp.dot(turned, mixed[:, :COLS], preferred_element_type=F32).astype(BF)
-        part_a[places] = block.reshape(2, 4, 112, COLS)
-        block = jnp.dot(turned, mixed[:, COLS:], preferred_element_type=F32).astype(BF)
-        part_b[places, :, :, : COLS - HEAD_DIM] = block.reshape(2, 4, 112, COLS - HEAD_DIM)
-        block = jnp.dot(normed[:, at].T, grad[...], preferred_element_type=F32).astype(BF)
-        part_b[places, :, :, COLS - HEAD_DIM :] = block.reshape(2, 4, 112, HEAD_DIM)
+        block = jnp.dot(upstream_turned[rows, :], mixed[:, :SPLIT], preferred_element_type=F32)
+        part_a[places, :, :, :SPLIT] = block.astype(BF).reshape(2, 4, 112, SPLIT)
+        block = jnp.dot(normed[:, at].T, grad[...], preferred_element_type=F32)
+        part_a[places, :, :, SPLIT:] = block.astype(BF).reshape(2, 4, 112, HEAD_DIM)
         return carry
 
-    lax.fori_loop(0, 4, products, 0)
-
-    def flow(size, place, ways, local, landing, hops):
-        nonlocal base
-        first = base
-        made = Flow(
-            size, place, *ways, local, lambda slot: landing.at[slot - first], sends, receives, base, hops
-        )
-        base += made.count
-        return made
-
-    z_halves = {(1, 0): 4, (-1, 1): 4, (1, 1): 3, (-1, 0): 3}
-    y_halves = {(1, 0): 2, (-1, 1): 2, (1, 1): 1, (-1, 0): 1}
-    z_whole = {(1, 0): 4, (-1, 0): 3}
-    y_whole = {(1, 0): 2, (-1, 0): 1}
-    a1 = flow(8, z, z_ways, lambda q, h: part_a.at[q, pl.ds(2 * h, 2)], land_a1, z_halves)
-    b1 = flow(4, y, y_ways, lambda q, h: part_b.at[pl.ds(4 * h, 4), q], land_b1, y_halves)
-    a2 = flow(4, y, y_ways, lambda q, h: part_a.at[z, q], land_a2, y_whole)
-    b2 = flow(8, z, z_ways, lambda q, h: part_b.at[q, y], land_b2, z_whole)
-    g1 = flow(8, z, z_ways, lambda q, h: part_g.at[q], land_g1, z_whole)
-    g2 = flow(4, y, y_ways, lambda q, h: part_g.at[z, q], land_g2, y_whole)
-
+    lax.fori_loop(0, 4, first_products, 0)
     a1.step(0)
-    b1.step(0)
     send_weight.wait_recv()
     send_grad.wait_recv()
 
-    def norm_back(index, total):
-        at = pl.ds(pl.multiple_of(index * BLOCK, BLOCK), BLOCK)
-        last_dims = (((1,), (1,)), ((), ()))
-        mine = lax.dot_general(grad[...], weight[at, :], last_dims, preferred_element_type=F32)
-        theirs = lax.dot_general(
-            grad_other[...], weight_other[at, :], last_dims, preferred_element_type=F32
-        )
-        both = mine.astype(BF).astype(F32) + theirs.astype(BF).astype(F32)
-        normed_grad[:, at] = both
-        term = both * inputs[:, at].astype(F32)
-        gain_row[:, at] = jnp.sum(term * wide(rms[...]), axis=0, keepdims=True)
-        term = term * gain[:, at]
-        return total + term[:, :128] + term[:, 128:]
-
-    total = lax.fori_loop(0, BLOCKS, norm_back, jnp.zeros((TOKENS, 128), F32))
-    mean = jnp.sum(total, axis=1, keepdims=True) / WIDTH
-    cubed = rms[...] * rms[...] * rms[...] * mean
-    normed_grad_scale = cubed
     outputs = []
     for pair in range(2):
         rows = pl.ds(128 * pair, 128)
-        slope = wide(normed_grad_scale[128 * pair : 128 * (pair + 1)])
+
+        def norm_back(index, total):
+            at = pl.ds(pl.multiple_of(index * BLOCK, BLOCK), BLOCK)
+            last_dims = (((1,), (1,)), ((), ()))
+            mine = lax.dot_general(
+                grad[rows, :], weight[at, :], last_dims, preferred_element_type=F32
+            )
+            theirs = lax.dot_general(
+                grad_other[rows, :], weight_other[at, :], last_dims, preferred_element_type=F32
+            )
+            both = mine.astype(BF).astype(F32) + theirs.astype(BF).astype(F32)
+            normed_grad[rows, at] = both
+            term = both * inputs[rows, at].astype(F32)
+            terms = jnp.sum(term * wide(rms[rows, :]), axis=0, keepdims=True)
+            gain_row[:, at] = terms if pair == 0 else gain_row[:, at] + terms
+            term = term * gain[:, at]
+            return total + term[:, :128] + term[:, 128:]
+
+        total = lax.fori_loop(0, BLOCKS, norm_back, jnp.zeros((128, 128), F32))
+        mean = jnp.sum(total, axis=1, keepdims=True) / WIDTH
+        scale = rms[rows, :]
+        slope = wide(scale * scale * scale * mean)
 
         def through(index, carry):
             at = pl.ds(pl.multiple_of(index * BLOCK, BLOCK), BLOCK)
@@ -492,44 +496,44 @@
         copy.start()
         return copy, jnp.where(x == 0, low, high)
 
+    g1.step(0)
     a1.step(1)
-    g1.step(0)
     b1.step(1)
+    a1.step(2)
     g1.step(1)
-    a1.step(2)
+    a1.step(3)
     g1.step(2)
-    a1.step(3)
-    g1.step(3)
     b1.finish()
     b2.step(0)
     a1.finish()
     a2.step(0)
+    g1.step(3)
+    b2.step(1)
+    a2.step(1)
     g1.finish()
     g2.step(0)
-    b2.step(1)
-    a2.step(1)
-    g2.step(1)
     b2.step(2)
     a2.finish()
     copy_a, own_a = exchange(0, part_a)
-    mixed_out[:, :COLS] = own_a
+    mixed_out[:, :SPLIT] = own_a[:, :SPLIT]
+    value_out[...] = own_a[:, SPLIT:]
+    g2.step(1)
+    b2.step(3)
     g2.finish()
     copy_g = last(2, part_g.at[z, y], last_g)
     copy_g.start()
-    b2.step(3)
     b2.finish()
     copy_b, own_b = exchange(1, part_b)
-    mixed_out[:, COLS:] = own_b[:, : COLS - HEAD_DIM]
-    value_out[...] = own_b[:, COLS - HEAD_DIM :]
+    mixed_out[:, SPLIT:] = own_b
     copy_a.wait_recv()
-    mixed_out[:, :COLS] += last_dst[0].astype(F32)
+    landed = last_dst[0].astype(F32)
+    mixed_out[:, :SPLIT] += landed[:, :SPLIT]
+    value_out[...] += landed[:, SPLIT:]
     copy_g.wait_recv()
     gain_total = part_g[z, y] + last_g[...]
     gain_out[...] = jnp.where(x == 0, gain_total[:, :56], gain_total[:, 56:112])
     copy_b.wait_recv()
-    landed = last_dst[1].astype(F32)
-    mixed_out[:, COLS:] += landed[:, : COLS - HEAD_DIM]
-    value_out[...] += landed[:, COLS - HEAD_DIM :]
+    mixed_out[:, SPLIT:] += last_dst[1].astype(F32)
     for made in (count_z, count_y, count_x, a1, b1, a2, b2, g1, g2):
         made.drain()
     for copy in (copy_a, copy_b, copy_g, send_weight, send_grad):
@@ -542,6 +546,31 @@
         send_head.wait_send()
         for send in send_below:
             send.wait_send()
+
+
+def copy_kernel(*refs):
+    sources, targets, sems = refs[:4], refs[4:8], refs[8]
+    copies = [
+        pltpu.make_async_copy(source, target, sems.at[index])
+        for index, (source, target) in enumerate(zip(sources, targets))
+    ]
+    for copy in copies:
+        copy.start()
+    for copy in copies:
+        copy.wait()
+
+
+def written_out(arrays):
+    vmem = pl.BlockSpec(memory_space=pltpu.VMEM)
+    hbm = pl.BlockSpec(memory_space=pl.ANY)
+    return pl.pallas_call(
+        copy_kernel,
+        out_shape=tuple(jax.ShapeDtypeStruct(array.shape, array.dtype) for array in arrays),
+        in_specs=[vmem] * 4,
+        out_specs=(hbm,) * 4,
+        scratch_shapes=[pltpu.SemaphoreType.DMA((4,))],
+        compiler_params=pltpu.CompilerParams(vmem_limit_bytes=4 * 1024 * 1024),
+    )(*arrays)
 
 
 def body(
@@ -555,10 +584,10 @@
     reference_logprob,
     sequence_bounds,
 ):
-    copies = 7 + 3 + 1 + 14 + 6 + 3 + 7 + 7 + 3 + 3
+    copies = 7 + 3 + 1 + 14 + 6 + 6 + 14 + 7 + 3 + 3
     vmem = pl.BlockSpec(memory_space=pltpu.VMEM)
     smem = pl.BlockSpec(memory_space=pltpu.SMEM)
-    hbm = pl.BlockSpec(memory_space=pl.ANY)
+    hbm = pl.BlockSpec(memory_space=pltpu.HBM)
     mixed_share, value_share, gain_share, own_output = pl.pallas_call(
         step_kernel,
         out_shape=(
@@ -568,7 +597,7 @@
             jax.ShapeDtypeStruct((2, LENGTH, WIDTH), BF),
         ),
         in_specs=[smem, smem, vmem, vmem, hbm, hbm, hbm, hbm, hbm],
-        out_specs=(vmem, vmem, vmem, hbm),
+        out_specs=(vmem, vmem, vmem, pl.BlockSpec(memory_space=pl.ANY)),
         scratch_shapes=[
             pltpu.VMEM((TOKENS, WIDTH), BF),
             pltpu.VMEM((4, HEADS * LENGTH, LENGTH), BF),
@@ -578,6 +607,7 @@
             pltpu.VMEM((2, LENGTH, WIDTH), BF),
             pltpu.VMEM((2, LENGTH, WIDTH), BF),
             pltpu.VMEM((TOKENS, WIDTH), BF),
+            pltpu.VMEM((WIDTH, TOKENS), BF),
             pltpu.VMEM((TOKENS, WIDTH), BF),
             pltpu.VMEM((TOKENS, WIDTH), BF),
             pltpu.VMEM((TOKENS, HEAD_DIM), BF),
@@ -597,8 +627,8 @@
             pltpu.VMEM((8, 4, 1, 128), F32),
             pltpu.VMEM((14, 2, 112, COLS), BF),
             pltpu.VMEM((6, 4, 112, COLS), BF),
-            pltpu.VMEM((3, 112, COLS), BF),
-            pltpu.VMEM((7, 112, COLS), BF),
+            pltpu.VMEM((6, 64, COLS), BF),
+            pltpu.VMEM((14, 64, COLS), BF),
             pltpu.VMEM((7, 4, 1, 128), F32),
             pltpu.VMEM((3, 1, 128), F32),
             pltpu.VMEM((2, 56, COLS), BF),
@@ -612,7 +642,7 @@
             pltpu.SemaphoreType.DMA((copies,)),
         ],
         compiler_params=pltpu.CompilerParams(
-            collective_id=0, has_side_effects=True, vmem_limit_bytes=60 * 1024 * 1024
+            collective_id=0, has_side_effects=True, vmem_limit_bytes=60_000_000
         ),
     )(
         sequence_bounds,
@@ -624,6 +654,9 @@
         value_weight[0],
         output_weight[0],
         head_grad.reshape(2, LENGTH, WIDTH),
+    )
+    mixed_share, value_share, gain_share, own_output = written_out(
+        (mixed_share, value_share, gain_share, own_output)
     )
     return (
         own_output.reshape(1, 2, 1, LENGTH, WIDTH),

time: 112 us -> 106 us (0.946)
  Pallas kernels: 105 us -> 101 us
  local copies, waits for them, and re-layouts: 6.31 us -> 3.52 us
    pallas_call x1, Pallas kernels: 105 us -> 100 us  [body(): pl.pallas_call(step_kernel, out_shape=(jax.ShapeDtypeStruct((56, HEADS *...]
    unnamed x4 -> x8, local copies, waits for them, and re-layouts: 6.31 us -> 3.52 us
where the time goes in v3:
time: 106 us; the launch traced here: 105 us
  Pallas kernels  101 us (95%)
  local copies, waits for them, and re-layouts  3.52 us (3%)
    pallas_call x1, Pallas kernels, body(): pl.pallas_call(step_kernel, out_shape=(jax.ShapeDtypeStruct((56, HEADS *...  100 us
    unnamed x8, local copies, waits for them, and re-layouts  3.52 us

profile of v3, /device:TPU:2, one launch (start us, length us, event | category | flops | bytes accessed | tf_op | source)
XLA Modules:
  0.0 105.3 jit_solution(12963666985455048197)
XLA Ops:
  0.6 100.1 %shard_map.120 = (f32[56,896]{1,0:T(8,128)}, f32[56,128]{1,0:T(8,128)}, f32[1,56]{1,0:T(1,128)}, bf16[2,64,3584]{2,1,0:T(8,128)(2,1)}) custom-call(s32[2,3]{1,0:T(2,128)} %bounds.1, f32[2,2]{1,0:T(2,128)} %reference.1, f32[2,2,64]{2,1,0:T(2,128)} %logprob.1, f32[1,3584]{1,0:T(1,128)} %gain.1, bf16[256,3584]{1,0:T(8,128)(2,1)} %bitcast.11, ...), custom_call_target="tpu_custom_call" | custom-call | tf_op jit(solution)/shard_map/pallas_call | solution.py:591
  100.7 0.0 copy-start
  100.7 1.2 %copy-done = bf16[2,64,3584]{2,1,0:T(8,128)(2,1)S(1)} copy-done((bf16[2,64,3584]{2,1,0:T(8,128)(2,1)S(1)}, bf16[2,64,3584]{2,1,0:T(8,128)(2,1)}, u32[]{:S(2)}) %copy-start) | copy-done | bytes 917528
  101.9 0.0 copy-start.1
  101.9 0.9 copy-done.1
  102.8 0.0 copy-start.2
  102.8 0.7 copy-done.2
  103.6 0.0 copy-start.3
  103.6 0.7 copy-done.3
  104.2 1.0 shard_map.121
Async XLA Ops:
  100.7 1.2 %copy-start = (bf16[2,64,3584]{2,1,0:T(8,128)(2,1)S(1)}, bf16[2,64,3584]{2,1,0:T(8,128)(2,1)}, u32[]{:S(2)}) copy-start(bf16[2,64,3584]{2,1,0:T(8,128)(2,1)} %get-tuple-element.15.refs_3_) | copy-start | bytes 2752516
  101.9 0.9 copy-start.1
  102.8 0.7 copy-start.2
  103.6 0.7 copy-start.3

commit v4 on v3

--- a/solution.py
+++ b/solution.py
@@ -118,6 +118,25 @@
             copy.wait_send()
 
 
+class Shares(Spread):
+    def __init__(self, size, place, device_at, local, landing, sends, receives, base):
+        self.own, self.landing = local.at[place], landing
+        self.count = size - 1
+        self.copies = []
+        for slot in range(self.count):
+            at = lax.rem(place + 1 + slot, size)
+            self.copies.append(
+                pltpu.make_async_remote_copy(
+                    src_ref=local.at[at],
+                    dst_ref=landing.at[slot],
+                    send_sem=sends.at[base + slot],
+                    recv_sem=receives.at[base + slot],
+                    device_id=device_at(at),
+                    device_id_type=MESH,
+                )
+            )
+
+
 WIDTH = 3584
 TOKENS = 256
 BLOCK = 256
@@ -131,19 +150,24 @@
 
 
 def step_kernel(
-    bounds,
-    reference,
-    logprob,
-    gain,
+    bounds_hbm,
+    reference_hbm,
+    logprob_hbm,
+    gain_hbm,
     inputs_hbm,
     pattern_hbm,
     value_hbm,
     output_hbm,
     head_hbm,
-    mixed_out,
-    value_out,
-    gain_out,
+    kept_out,
+    landed_out,
+    gain_kept_out,
+    gain_landed_out,
     cotangent_out,
+    bounds,
+    reference,
+    logprob,
+    gain,
     inputs,
     pattern,
     weight,
@@ -162,6 +186,7 @@
     grad_other,
     normed_grad,
     rms,
+    slopes,
     gain_row,
     counts,
     land_cz,
@@ -170,15 +195,18 @@
     part_a,
     part_b,
     part_g,
+    part_h,
     land_a1,
+    land_v1,
     land_b1,
     land_a2,
     land_b2,
     land_g1,
     land_g2,
     last_src,
-    last_dst,
-    last_g,
+    kept,
+    gain_last,
+    gain_kept,
     load_sems,
     pass_sends,
     pass_receives,
@@ -205,21 +233,6 @@
     cross = (pipe, z * 8 + y * 2 + 1 - x, 1 - tensor)
     partner = (1 - pipe, dp, tensor)
 
-    loads = {
-        name: pltpu.make_async_copy(source, target, load_sems.at[index])
-        for index, (name, source, target) in enumerate(
-            (
-                ("inputs", inputs_hbm, inputs),
-                ("weight", value_hbm, weight),
-                ("pattern", pattern_hbm, pattern),
-                ("head", head_hbm, head_own),
-                ("output", output_hbm, weight_out),
-            )
-        )
-    }
-    for load in loads.values():
-        load.start()
-
     def token_rows(pair, which):
         lanes = lax.broadcasted_iota(jnp.int32, (1, LENGTH), 1)
         rows = lax.broadcasted_iota(jnp.int32, (LENGTH, 1), 0)
@@ -228,18 +241,41 @@
         column_mask = ((rows >= first) & (rows < end)).astype(F32)
         return row_mask, column_mask
 
+    barrier = pltpu.get_barrier_semaphore()
+    z_others = [device(lax.rem(z + step, 8), y, x) for step in range(1, 8)]
+    y_others = [device(z, lax.rem(y + step, 4), x) for step in range(1, 4)]
+    for neighbour in (*z_others, *y_others, x_way, peer, cross, partner):
+        pl.semaphore_signal(barrier, inc=1, device_id=neighbour, device_id_type=MESH)
+    loads = {
+        name: pltpu.make_async_copy(source, target, load_sems.at[index])
+        for index, (name, source, target) in enumerate(
+            (
+                ("head", head_hbm, head_own),
+                ("bounds", bounds_hbm, bounds),
+                ("reference", reference_hbm, reference),
+                ("logprob", logprob_hbm, logprob),
+                ("gain", gain_hbm, gain),
+                ("inputs", inputs_hbm, inputs),
+                ("weight", value_hbm, weight),
+                ("pattern", pattern_hbm, pattern),
+                ("output", output_hbm, weight_out),
+            )
+        )
+    }
+    for load in loads.values():
+        load.start()
+
+    for name in ("bounds", "reference", "logprob", "gain"):
+        loads[name].wait()
     own_count = jnp.zeros((1, 1), F32)
     for pair in range(2):
         own_count = own_count + jnp.sum(token_rows(pair, 0)[0], axis=1, keepdims=True)
     counts[0] = jnp.broadcast_to(own_count, (1, 128))
     part_g[...] = jnp.zeros_like(part_g)
-
-    barrier = pltpu.get_barrier_semaphore()
-    z_others = [device(lax.rem(z + step, 8), y, x) for step in range(1, 8)]
-    y_others = [device(z, lax.rem(y + step, 4), x) for step in range(1, 4)]
-    for neighbour in (*z_others, *y_others, x_way, peer, cross, partner):
-        pl.semaphore_signal(barrier, inc=1, device_id=neighbour, device_id_type=MESH)
+    gain_last[...] = jnp.zeros_like(gain_last)
+    gain_kept[...] = jnp.zeros_like(gain_kept)
     pl.semaphore_wait(barrier, 14)
+    loads["head"].wait()
 
     def passing(index, source, target, to):
         return pltpu.make_async_remote_copy(
@@ -251,18 +287,14 @@
             device_id_type=MESH,
         )
 
-    send_head = passing(0, head_hbm, head_other, peer)
-    send_weight = passing(1, value_hbm, weight_other, cross)
+    send_head = passing(0, head_own, head_other, peer)
+    send_weight = passing(1, weight, weight_other, cross)
     send_grad = passing(2, grad, grad_other, peer)
     send_below = [
         passing(3 + pair, below.at[pl.ds(128 * pair, 128)], upstream.at[pl.ds(128 * pair, 128)], partner)
         for pair in range(2)
     ]
 
-    @pl.when(pipe == 1)
-    def _():
-        send_head.start()
-
     base = 0
 
     def spread(size, place, device_at, own, landing):
@@ -271,11 +303,15 @@
         base += made.count
         return made
 
-    count_z = spread(8, z, lambda at: device(at, y, x), counts.at[0], land_cz)
-    count_y = spread(4, y, lambda at: device(z, at, x), counts.at[1], land_cy)
-    count_x = spread(2, x, lambda at: device(z, y, at), counts.at[2], land_cx)
-
-    count_z.start()
+    count_x = spread(2, x, lambda at: device(z, y, at), counts.at[0], land_cx)
+    count_z = spread(8, z, lambda at: device(at, y, x), counts.at[1], land_cz)
+    count_y = spread(4, y, lambda at: device(z, at, x), counts.at[2], land_cy)
+    count_x.start()
+
+    @pl.when(pipe == 1)
+    def _():
+        send_head.start()
+
     loads["inputs"].wait()
 
     def square(index, total):
@@ -287,6 +323,8 @@
     total = lax.fori_loop(0, BLOCKS, square, jnp.zeros((TOKENS, 128), F32))
     mean = jnp.sum(total, axis=1, keepdims=True) / WIDTH
     rms[...] = jnp.broadcast_to(lax.rsqrt(mean + EPSILON), (TOKENS, 128))
+    counts[1] = count_x.finish()
+    count_z.start()
     loads["weight"].wait()
 
     def project(index, total):
@@ -297,8 +335,6 @@
 
     total = lax.fori_loop(0, BLOCKS, project, jnp.zeros((TOKENS, 128), F32))
     values[...] = total.astype(BF)
-    counts[1] = count_z.finish()
-    count_y.start()
     loads["pattern"].wait()
 
     def mix(index, carry):
@@ -308,12 +344,10 @@
             mixed[rows, head * 128 : (head + 1) * 128] = block[head * LENGTH : (head + 1) * LENGTH]
         return carry
 
-    lax.fori_loop(0, 2, mix, 0)
-    counts[2] = count_y.finish()
-    count_x.start()
-    lax.fori_loop(2, 4, mix, 0)
-    loads["head"].wait()
-    total_count = count_x.finish()[:, :1]
+    counts[2] = count_z.finish()
+    count_y.start()
+    lax.fori_loop(0, 4, mix, 0)
+    total_count = count_y.finish()[:, :1]
     loads["output"].wait()
 
     @pl.when(pipe == 1)
@@ -337,8 +371,9 @@
             upstream[rows, :] = (mine * head_own[pair].astype(F32)).astype(BF)
             if pair == 0:
                 kept = theirs
+        send_head.wait_send()
+        send_weight.start()
         send_head.wait_recv()
-        send_weight.start()
         for pair, theirs in enumerate((kept, theirs)):
             rows = pl.ds(pl.multiple_of((2 * pair + 1 - tensor) * LENGTH, LENGTH), LENGTH)
             upstream[rows, :] = (theirs * head_other[pair].astype(F32)).astype(BF)
@@ -364,24 +399,57 @@
     z_whole = {(1, 0): 4, (-1, 0): 3}
     y_whole = {(1, 0): 2, (-1, 0): 1}
     rows_of = (pl.ds(0, 64), pl.ds(64, 48))
-    a1 = flow(8, z, z_ways, lambda q, h: part_a.at[q, pl.ds(2 * h, 2)], land_a1, z_halves)
+    a1 = flow(
+        8, z, z_ways, lambda q, h: part_a.at[q, pl.ds(2 * h, 2), :, pl.ds(0, SPLIT)], land_a1, z_halves
+    )
+    v1 = flow(
+        8,
+        z,
+        z_ways,
+        lambda q, h: part_a.at[q, pl.ds(2 * h, 2), :, pl.ds(SPLIT, HEAD_DIM)],
+        land_v1,
+        z_halves,
+    )
     b1 = flow(4, y, y_ways, lambda q, h: part_b.at[pl.ds(4 * h, 4), q], land_b1, y_halves)
     a2 = flow(4, y, y_ways, lambda q, h: part_a.at[z, q, rows_of[h]], land_a2, y_halves)
     b2 = flow(8, z, z_ways, lambda q, h: part_b.at[q, y, rows_of[h]], land_b2, z_halves)
-    g1 = flow(8, z, z_ways, lambda q, h: part_g.at[q], land_g1, z_whole)
-    g2 = flow(4, y, y_ways, lambda q, h: part_g.at[z, q], land_g2, y_whole)
+
+    def shares(size, place, device_at, local, landing):
+        nonlocal base
+        made = Shares(size, place, device_at, local, landing, sends, receives, base)
+        base += made.count
+        return made
+
+    g1 = shares(8, z, lambda at: device(at, y, x), part_g, land_g1)
+    g2 = shares(4, y, lambda at: device(z, at, x), part_h, land_g2)
 
     def later_products(index, carry):
         at = pl.ds(pl.multiple_of(index * 896, 128), 896)
-        rows = pl.ds(pl.multiple_of(index * 896, 128), 896)
         places = pl.ds(2 * index, 2)
-        upstream_turned[rows, :] = upstream[:, at].T
-        block = jnp.dot(upstream_turned[rows, :], mixed[:, SPLIT:], preferred_element_type=F32)
+        turned = upstream[:, at].T
+        upstream_turned[at, :] = turned
+        block = jnp.dot(turned, mixed[:, SPLIT:], preferred_element_type=F32)
         part_b[places] = block.astype(BF).reshape(2, 4, 112, COLS)
         return carry
 
+    def first_products(index, carry):
+        at = pl.ds(pl.multiple_of(index * 896, 128), 896)
+        places = pl.ds(2 * index, 2)
+        block = jnp.dot(upstream_turned[at, :], mixed[:, :SPLIT], preferred_element_type=F32)
+        part_a[places, :, :, :SPLIT] = block.astype(BF).reshape(2, 4, 112, SPLIT)
+        return carry
+
+    def value_products(index, carry):
+        at = pl.ds(pl.multiple_of(index * 896, 128), 896)
+        places = pl.ds(2 * index, 2)
+        block = jnp.dot(normed[:, at].T, grad[...], preferred_element_type=F32)
+        part_a[places, :, :, SPLIT:] = block.astype(BF).reshape(2, 4, 112, HEAD_DIM)
+        return carry
+
     lax.fori_loop(0, 4, later_products, 0)
     b1.step(0)
+    lax.fori_loop(0, 4, first_products, 0)
+    a1.step(0)
 
     def heads_back(first, count):
         rows = pl.ds(pl.multiple_of(first * 128, 128), count * 128)
@@ -402,10 +470,6 @@
     lax.fori_loop(0, 3, two_heads, 0)
     heads_back(6, 1)
 
-    @pl.when(pipe == 1)
-    def _():
-        pl.semaphore_signal(go, inc=1, device_id=partner, device_id_type=MESH)
-
     def unmix(index, carry):
         rows = pl.ds(pl.multiple_of(index * LENGTH, LENGTH), LENGTH)
         grad[rows, :] = lax.dot_general(
@@ -416,67 +480,94 @@
     lax.fori_loop(0, 4, unmix, 0)
     send_grad.start()
 
-    def first_products(index, carry):
-        at = pl.ds(pl.multiple_of(index * 896, 128), 896)
-        rows = pl.ds(pl.multiple_of(index * 896, 128), 896)
-        places = pl.ds(2 * index, 2)
-        block = jnp.dot(upstream_turned[rows, :], mixed[:, :SPLIT], preferred_element_type=F32)
-        part_a[places, :, :, :SPLIT] = block.astype(BF).reshape(2, 4, 112, SPLIT)
-        block = jnp.dot(normed[:, at].T, grad[...], preferred_element_type=F32)
-        part_a[places, :, :, SPLIT:] = block.astype(BF).reshape(2, 4, 112, HEAD_DIM)
-        return carry
-
-    lax.fori_loop(0, 4, first_products, 0)
-    a1.step(0)
-    send_weight.wait_recv()
-    send_grad.wait_recv()
-
+    lax.fori_loop(0, 4, value_products, 0)
+    v1.step(0)
     outputs = []
     for pair in range(2):
+        own_rows = pl.ds(pl.multiple_of((2 * pair + tensor) * LENGTH, LENGTH), LENGTH)
+        outputs.append(
+            pltpu.make_async_copy(below.at[own_rows], cotangent_out.at[pair], load_sems.at[9 + pair])
+        )
+
+    def norm_back(index, total):
+        at = pl.ds(pl.multiple_of(index * BLOCK, BLOCK), BLOCK)
+        last_dims = (((1,), (1,)), ((), ()))
+        mine = lax.dot_general(grad[...], weight[at, :], last_dims, preferred_element_type=F32)
+        theirs = lax.dot_general(
+            grad_other[...], weight_other[at, :], last_dims, preferred_element_type=F32
+        )
+        both = mine.astype(BF).astype(F32) + theirs.astype(BF).astype(F32)
+        normed_grad[:, at] = both
+        term = both * inputs[:, at].astype(F32)
+        gain_row[:, at] = jnp.sum(term * wide(rms[...]), axis=0, keepdims=True)
+        term = term * gain[:, at]
+        return total + term[:, :128] + term[:, 128:]
+
+    def norm_pass():
+        send_grad.wait_recv()
+        total = lax.fori_loop(0, BLOCKS, norm_back, jnp.zeros((TOKENS, 128), F32), unroll=2)
+        mean = jnp.sum(total, axis=1, keepdims=True) / WIDTH
+        slopes[...] = rms[...] * rms[...] * rms[...] * mean
+        for place in range(32):
+            part_g[place // 4, place % 4, :, :112] = gain_row[:, 112 * place : 112 * (place + 1)]
+        g1.start()
+
+    def below_pass(pair):
         rows = pl.ds(128 * pair, 128)
-
-        def norm_back(index, total):
-            at = pl.ds(pl.multiple_of(index * BLOCK, BLOCK), BLOCK)
-            last_dims = (((1,), (1,)), ((), ()))
-            mine = lax.dot_general(
-                grad[rows, :], weight[at, :], last_dims, preferred_element_type=F32
-            )
-            theirs = lax.dot_general(
-                grad_other[rows, :], weight_other[at, :], last_dims, preferred_element_type=F32
-            )
-            both = mine.astype(BF).astype(F32) + theirs.astype(BF).astype(F32)
-            normed_grad[rows, at] = both
-            term = both * inputs[rows, at].astype(F32)
-            terms = jnp.sum(term * wide(rms[rows, :]), axis=0, keepdims=True)
-            gain_row[:, at] = terms if pair == 0 else gain_row[:, at] + terms
-            term = term * gain[:, at]
-            return total + term[:, :128] + term[:, 128:]
-
-        total = lax.fori_loop(0, BLOCKS, norm_back, jnp.zeros((128, 128), F32))
-        mean = jnp.sum(total, axis=1, keepdims=True) / WIDTH
-        scale = rms[rows, :]
-        slope = wide(scale * scale * scale * mean)
 
         def through(index, carry):
             at = pl.ds(pl.multiple_of(index * BLOCK, BLOCK), BLOCK)
             scaled = normed_grad[rows, at] * gain[:, at]
+            slope = wide(slopes[rows, :])
             change = wide(rms[rows, :]) * scaled - inputs[rows, at].astype(F32) * slope
             below[rows, at] = (upstream[rows, at].astype(F32) + change).astype(BF)
             return carry
 
         lax.fori_loop(0, BLOCKS, through, 0)
 
-        @pl.when(pipe == 1)
-        def _():
+    b1.step(1)
+    a1.step(1)
+
+    @pl.when(pipe == 1)
+    def _():
+        send_weight.wait_recv()
+        pl.semaphore_signal(go, inc=1, device_id=partner, device_id_type=MESH)
+        norm_pass()
+        for pair in range(2):
+            below_pass(pair)
             send_below[pair].start()
-
-        own = pl.ds(pl.multiple_of((2 * pair + tensor) * LENGTH, LENGTH), LENGTH)
-        output = pltpu.make_async_copy(below.at[own], cotangent_out.at[pair], load_sems.at[5 + pair])
-        output.start()
-        outputs.append(output)
-
-    for place in range(32):
-        part_g[place // 4, place % 4, :, :112] = gain_row[:, 112 * place : 112 * (place + 1)]
+            outputs[pair].start()
+
+    v1.step(1)
+
+    @pl.when(pipe == 0)
+    def _():
+        send_weight.wait_recv()
+        norm_pass()
+
+    a1.step(2)
+    b1.finish()
+    b2.step(0)
+    v1.step(2)
+    a1.step(3)
+    b2.step(1)
+    v1.step(3)
+
+    @pl.when(pipe == 0)
+    def _():
+        for pair in range(2):
+            below_pass(pair)
+            outputs[pair].start()
+
+    b2.step(2)
+    a1.finish()
+    v1.finish()
+    a2.step(0)
+    part_h[...] = g1.finish()
+    g2.start()
+    b2.step(3)
+    a2.step(1)
+    b2.finish()
 
     def last(index, source, target):
         return pltpu.make_async_remote_copy(
@@ -488,88 +579,121 @@
             device_id_type=MESH,
         )
 
+    finals = []
+
     def exchange(index, part):
         total = part[z, y].astype(F32)
         low, high = total[:56], total[56:]
         last_src[index] = jnp.where(x == 0, high, low).astype(BF)
-        copy = last(index, last_src.at[index], last_dst.at[index])
+        copy = last(index, last_src.at[index], landed_out.at[index])
         copy.start()
-        return copy, jnp.where(x == 0, low, high)
-
-    g1.step(0)
-    a1.step(1)
-    b1.step(1)
-    a1.step(2)
-    g1.step(1)
-    a1.step(3)
-    g1.step(2)
-    b1.finish()
-    b2.step(0)
-    a1.finish()
-    a2.step(0)
-    g1.step(3)
-    b2.step(1)
-    a2.step(1)
-    g1.finish()
-    g2.step(0)
-    b2.step(2)
+        finals.append(copy)
+        kept[index] = jnp.where(x == 0, low, high)
+        keep = pltpu.make_async_copy(kept.at[index], kept_out.at[index], load_sems.at[11 + index])
+        keep.start()
+        outputs.append(keep)
+
+    exchange(1, part_b)
+    gain_total = g2.finish()
+    low, high = gain_total[:, :56], gain_total[:, 56:112]
+    gain_last[:, :56] = jnp.where(x == 0, high, low)
+    gain_copy = last(2, gain_last, gain_landed_out)
+    gain_copy.start()
+    finals.append(gain_copy)
+    gain_kept[:, :56] = jnp.where(x == 0, low, high)
+    gain_keep = pltpu.make_async_copy(gain_kept, gain_kept_out, load_sems.at[13])
+    gain_keep.start()
+    outputs.append(gain_keep)
     a2.finish()
-    copy_a, own_a = exchange(0, part_a)
-    mixed_out[:, :SPLIT] = own_a[:, :SPLIT]
-    value_out[...] = own_a[:, SPLIT:]
-    g2.step(1)
-    b2.step(3)
-    g2.finish()
-    copy_g = last(2, part_g.at[z, y], last_g)
-    copy_g.start()
-    b2.finish()
-    copy_b, own_b = exchange(1, part_b)
-    mixed_out[:, SPLIT:] = own_b
-    copy_a.wait_recv()
-    landed = last_dst[0].astype(F32)
-    mixed_out[:, :SPLIT] += landed[:, :SPLIT]
-    value_out[...] += landed[:, SPLIT:]
-    copy_g.wait_recv()
-    gain_total = part_g[z, y] + last_g[...]
-    gain_out[...] = jnp.where(x == 0, gain_total[:, :56], gain_total[:, 56:112])
-    copy_b.wait_recv()
-    mixed_out[:, SPLIT:] += last_dst[1].astype(F32)
-    for made in (count_z, count_y, count_x, a1, b1, a2, b2, g1, g2):
+    exchange(0, part_a)
+    for copy in finals:
+        copy.wait_recv()
+    for made in (count_z, count_y, count_x, a1, v1, b1, a2, b2, g1, g2):
         made.drain()
-    for copy in (copy_a, copy_b, copy_g, send_weight, send_grad):
+    for copy in (*finals, send_weight, send_grad):
         copy.wait_send()
     for output in outputs:
         output.wait()
 
     @pl.when(pipe == 1)
     def _():
-        send_head.wait_send()
         for send in send_below:
             send.wait_send()
 
 
-def copy_kernel(*refs):
-    sources, targets, sems = refs[:4], refs[4:8], refs[8]
-    copies = [
-        pltpu.make_async_copy(source, target, sems.at[index])
-        for index, (source, target) in enumerate(zip(sources, targets))
+def last_kernel(
+    kept_hbm,
+    landed_hbm,
+    gain_kept_hbm,
+    gain_landed_hbm,
+    cotangent_hbm,
+    mixed_hbm,
+    value_hbm,
+    gain_hbm,
+    cotangent_out,
+    kept,
+    landed,
+    gain_kept,
+    gain_landed,
+    cotangent,
+    mixed,
+    value,
+    gain,
+    load_sems,
+    store_sems,
+):
+    loads = [
+        pltpu.make_async_copy(source, buffer, load_sems.at[index])
+        for index, (source, buffer) in enumerate(
+            (
+                (kept_hbm, kept),
+                (landed_hbm, landed),
+                (gain_kept_hbm, gain_kept),
+                (gain_landed_hbm, gain_landed),
+                (cotangent_hbm, cotangent),
+            )
+        )
     ]
-    for copy in copies:
-        copy.start()
-    for copy in copies:
-        copy.wait()
+    stores = [
+        pltpu.make_async_copy(buffer, target, store_sems.at[index])
+        for index, (buffer, target) in enumerate(
+            ((mixed, mixed_hbm), (value, value_hbm), (gain, gain_hbm), (cotangent, cotangent_out))
+        )
+    ]
+    for load in loads:
+        load.start()
+    for load in loads[:4]:
+        load.wait()
+    total = kept[0] + landed[0].astype(F32)
+    mixed[:, :SPLIT] = total[:, :SPLIT]
+    value[...] = total[:, SPLIT:]
+    mixed[:, SPLIT:] = kept[1] + landed[1].astype(F32)
+    gain[...] = gain_kept[:, :56] + gain_landed[:, :56]
+    for store in stores[:3]:
+        store.start()
+    loads[4].wait()
+    stores[3].start()
+    for store in stores:
+        store.wait()
 
 
 def written_out(arrays):
-    vmem = pl.BlockSpec(memory_space=pltpu.VMEM)
     hbm = pl.BlockSpec(memory_space=pl.ANY)
+    shapes = (
+        jax.ShapeDtypeStruct((56, HEADS * HEAD_DIM), F32),
+        jax.ShapeDtypeStruct((56, HEAD_DIM), F32),
+        jax.ShapeDtypeStruct((1, 56), F32),
+        jax.ShapeDtypeStruct((2, LENGTH, WIDTH), BF),
+    )
     return pl.pallas_call(
-        copy_kernel,
-        out_shape=tuple(jax.ShapeDtypeStruct(array.shape, array.dtype) for array in arrays),
-        in_specs=[vmem] * 4,
+        last_kernel,
+        out_shape=shapes,
+        in_specs=[hbm] * 5,
         out_specs=(hbm,) * 4,
-        scratch_shapes=[pltpu.SemaphoreType.DMA((4,))],
-        compiler_params=pltpu.CompilerParams(vmem_limit_bytes=4 * 1024 * 1024),
+        scratch_shapes=[pltpu.VMEM(array.shape, array.dtype) for array in arrays]
+        + [pltpu.VMEM(shape.shape, shape.dtype) for shape in shapes[:3]]
+        + [pltpu.SemaphoreType.DMA((5,)), pltpu.SemaphoreType.DMA((4,))],
+        compiler_params=pltpu.CompilerParams(vmem_limit_bytes=60_000_000),
     )(*arrays)
 
 
@@ -584,21 +708,24 @@
     reference_logprob,
     sequence_bounds,
 ):
-    copies = 7 + 3 + 1 + 14 + 6 + 6 + 14 + 7 + 3 + 3
-    vmem = pl.BlockSpec(memory_space=pltpu.VMEM)
-    smem = pl.BlockSpec(memory_space=pltpu.SMEM)
-    hbm = pl.BlockSpec(memory_space=pltpu.HBM)
-    mixed_share, value_share, gain_share, own_output = pl.pallas_call(
+    copies = 7 + 3 + 1 + 14 + 14 + 6 + 6 + 14 + 7 + 3 + 3
+    hbm = pl.BlockSpec(memory_space=pl.ANY)
+    results = pl.pallas_call(
         step_kernel,
         out_shape=(
-            jax.ShapeDtypeStruct((56, HEADS * HEAD_DIM), F32),
-            jax.ShapeDtypeStruct((56, HEAD_DIM), F32),
-            jax.ShapeDtypeStruct((1, 56), F32),
+            jax.ShapeDtypeStruct((2, 56, COLS), F32),
+            jax.ShapeDtypeStruct((2, 56, COLS), BF),
+            jax.ShapeDtypeStruct((1, 128), F32),
+            jax.ShapeDtypeStruct((1, 128), F32),
             jax.ShapeDtypeStruct((2, LENGTH, WIDTH), BF),
         ),
-        in_specs=[smem, smem, vmem, vmem, hbm, hbm, hbm, hbm, hbm],
-        out_specs=(vmem, vmem, vmem, pl.BlockSpec(memory_space=pl.ANY)),
+        in_specs=[hbm] * 9,
+        out_specs=(hbm,) * 5,
         scratch_shapes=[
+            pltpu.SMEM((2, 3), jnp.int32),
+            pltpu.SMEM((2, 2), F32),
+            pltpu.VMEM((2, 2, LENGTH), F32),
+            pltpu.VMEM((1, WIDTH), F32),
             pltpu.VMEM((TOKENS, WIDTH), BF),
             pltpu.VMEM((4, HEADS * LENGTH, LENGTH), BF),
             pltpu.VMEM((WIDTH, HEAD_DIM), BF),
@@ -617,6 +744,7 @@
             pltpu.VMEM((TOKENS, HEAD_DIM), BF),
             pltpu.VMEM((TOKENS, WIDTH), F32),
             pltpu.VMEM((TOKENS, 128), F32),
+            pltpu.VMEM((TOKENS, 128), F32),
             pltpu.VMEM((1, WIDTH), F32),
             pltpu.VMEM((3, 1, 128), F32),
             pltpu.VMEM((7, 1, 128), F32),
@@ -625,16 +753,19 @@
             pltpu.VMEM((8, 4, 112, COLS), BF),
             pltpu.VMEM((8, 4, 112, COLS), BF),
             pltpu.VMEM((8, 4, 1, 128), F32),
-            pltpu.VMEM((14, 2, 112, COLS), BF),
+            pltpu.VMEM((4, 1, 128), F32),
+            pltpu.VMEM((14, 2, 112, SPLIT), BF),
+            pltpu.VMEM((14, 2, 112, HEAD_DIM), BF),
             pltpu.VMEM((6, 4, 112, COLS), BF),
             pltpu.VMEM((6, 64, COLS), BF),
             pltpu.VMEM((14, 64, COLS), BF),
             pltpu.VMEM((7, 4, 1, 128), F32),
             pltpu.VMEM((3, 1, 128), F32),
             pltpu.VMEM((2, 56, COLS), BF),
-            pltpu.VMEM((2, 56, COLS), BF),
+            pltpu.VMEM((2, 56, COLS), F32),
             pltpu.VMEM((1, 128), F32),
-            pltpu.SemaphoreType.DMA((7,)),
+            pltpu.VMEM((1, 128), F32),
+            pltpu.SemaphoreType.DMA((14,)),
             pltpu.SemaphoreType.DMA((5,)),
             pltpu.SemaphoreType.DMA((5,)),
             pltpu.SemaphoreType.REGULAR,
@@ -655,9 +786,7 @@
         output_weight[0],
         head_grad.reshape(2, LENGTH, WIDTH),
     )
-    mixed_share, value_share, gain_share, own_output = written_out(
-        (mixed_share, value_share, gain_share, own_output)
-    )
+    mixed_share, value_share, gain_share, own_output = written_out(results)
     return (
         own_output.reshape(1, 2, 1, LENGTH, WIDTH),
         value_share[None],

time: 106 us -> 86 us (0.81)
  Pallas kernels: 101 us -> 85.3 us
  local copies, waits for them, and re-layouts: 3.52 us -> 0 us
    pallas_call x2, Pallas kernels: 101 us -> 85.3 us  [the longest x1 82.9 us: body(): pl.pallas_call(step_kernel, out_shape=(jax.ShapeDtypeStruct((2, 56, COLS)...]
    unnamed x8 -> x0, local copies, waits for them, and re-layouts: 3.52 us -> none
where the time goes in v4:
time: 86 us; the launch traced here: 85.9 us
  Pallas kernels  85.3 us (99%)
    pallas_call x1, Pallas kernels, body(): pl.pallas_call(step_kernel, out_shape=(jax.ShapeDtypeStruct((2, 56, COLS)...  82.9 us
    pallas_call x1, Pallas kernels, written_out(): pl.pallas_call(last_kernel, out_shape=shapes, in_specs=[hbm] * 5, out_spe...  2.37 us

profile of v4, /device:TPU:2, one launch (start us, length us, event | category | flops | bytes accessed | tf_op | source)
XLA Modules:
  0.0 85.9 jit_solution(1886176743547254297)
XLA Ops:
  0.6 82.9 %shard_map.120 = (f32[2,56,512]{2,1,0:T(8,128)}, bf16[2,56,512]{2,1,0:T(8,128)(2,1)}, f32[1,128]{1,0:T(1,128)}, f32[1,128]{1,0:T(1,128)}, bf16[2,64,3584]{2,1,0:T(8,128)(2,1)}) custom-call(s32[2,3]{1,0:T(2,128)} %bounds_hbm.1, f32[2,2]{1,0:T(2,128)} %reference_hbm.1, f32[2,2,64]{2,1,0:T(2,128)} %logprob_hbm.1, f32[1,3584]{1,0:T(1,128)} %gain_hbm.1, ...), custom_call_target="tpu_custom_call" | custom-call | tf_op jit(solution)/shard_map/pallas_call | solution.py:713
  83.5 2.4 %shard_map.121 = (f32[56,896]{1,0:T(8,128)}, f32[56,128]{1,0:T(8,128)}, f32[1,56]{1,0:T(1,128)}, bf16[2,64,3584]{2,1,0:T(8,128)(2,1)}) custom-call(f32[2,56,512]{2,1,0:T(8,128)} %get-tuple-element.13.kept_hbm, bf16[2,56,512]{2,1,0:T(8,128)(2,1)} %get-tuple-element.14.landed_hbm, f32[1,128]{1,0:T(1,128)} %get-tuple-element.15.gain_kept_hbm, ...), custom_call_target="tpu_custom_call" | custom-call | tf_op jit(solution)/shard_map/pallas_call | solution.py:688

commit v5 on v4

--- a/solution.py
+++ b/solution.py
@@ -16,62 +16,76 @@
 F32 = jnp.float32
 COLS = 512
 SPLIT = 384
+CROSS = 128
+NEAR = SPLIT - CROSS + HEAD_DIM
 
 
 class Flow:
-    def __init__(self, size, place, ahead, behind, local, landing, sends, receives, base, hops):
-        self.size, self.place = size, place
+    def __init__(self, size, place, ahead, behind, local, landing, sends, receives, bases, hops):
+        self.place, self.local, self.landing, self.hops = place, local, landing, hops
         self.target = {1: ahead, -1: behind}
-        self.local, self.landing = local, landing
-        self.sends, self.receives = sends, receives
-        self.hops = hops
         self.slot = {}
         for (way, half), count in hops.items():
             for step in range(count):
-                self.slot[way, half, step] = base + len(self.slot)
+                self.slot[way, half, step] = len(self.slot)
         self.count = len(self.slot)
-        self.copies = {}
-
-    def copy(self, way, half, step):
-        slot = self.slot[way, half, step]
-        chunk = lax.rem(self.place + way * (self.hops[way, half] - step) + self.size, self.size)
-        source = self.local(chunk, half)
-        return chunk, pltpu.make_async_remote_copy(
-            src_ref=source,
-            dst_ref=self.landed(slot, source),
-            send_sem=self.sends.at[slot],
-            recv_sem=self.receives.at[slot],
-            device_id=self.target[way],
-            device_id_type=MESH,
-        )
+        self.halves = 1 + max(half for _, half in hops)
+        self.copies, self.targets = {}, {}
+        for (way, half, step), slot in self.slot.items():
+            chunk = lax.rem(place + way * (hops[way, half] - step) + size, size)
+            source = self.targets[way, half, step] = local(chunk, half)
+            self.copies[way, half, step] = pltpu.make_async_remote_copy(
+                src_ref=source,
+                dst_ref=self.landed(slot, source),
+                send_sem=sends.at[bases[0] + half],
+                recv_sem=receives.at[bases[1] + slot],
+                device_id=self.target[way],
+                device_id_type=MESH,
+            )
+        self.drains = []
+        for half in range(self.halves):
+            sent = sum(count for (_, of), count in hops.items() if of == half)
+            like = local(place, half)
+            whole = landing.at[pl.ds(0, sent)]
+            if landing.shape[1] != like.shape[0]:
+                whole = landing.at[pl.ds(0, sent), pl.ds(0, like.shape[0])]
+            self.drains.append(waiting(whole, sends.at[bases[0] + half], receives.at[bases[1]], ahead))
 
     def landed(self, slot, like):
-        landing = self.landing(slot)
+        landing = self.landing.at[slot]
         if landing.shape == like.shape:
             return landing
         return landing.at[pl.ds(0, like.shape[0])]
 
-    def collect(self, way, half, step, chunk):
+    def collect(self, way, half, step, target):
         self.copies[way, half, step].wait_recv()
-        target = self.local(chunk, half)
         add_into(target, self.landed(self.slot[way, half, step], target))
 
     def step(self, step):
         for way, half in self.hops:
             if step < self.hops[way, half]:
-                chunk, copy = self.copy(way, half, step)
                 if step:
-                    self.collect(way, half, step - 1, chunk)
-                copy.start()
-                self.copies[way, half, step] = copy
+                    self.collect(way, half, step - 1, self.targets[way, half, step])
+                self.copies[way, half, step].start()
 
     def finish(self):
         for (way, half), count in self.hops.items():
-            self.collect(way, half, count - 1, self.place)
+            self.collect(way, half, count - 1, self.local(self.place, half))
 
     def drain(self):
-        for copy in self.copies.values():
+        for copy in self.drains:
             copy.wait_send()
+
+
+def waiting(whole, send_sem, recv_sem, device):
+    return pltpu.make_async_remote_copy(
+        src_ref=whole,
+        dst_ref=whole,
+        send_sem=send_sem,
+        recv_sem=recv_sem,
+        device_id=device,
+        device_id_type=MESH,
+    )
 
 
 def add_into(target, landed):
@@ -87,54 +101,37 @@
 
 
 class Spread:
-    def __init__(self, size, place, device_at, own, landing, sends, receives, base):
+    def __init__(self, size, place, device_at, own, share_at, landing, sends, receives, bases):
         self.own, self.landing = own, landing
-        self.count = size - 1
-        self.copies = [
-            pltpu.make_async_remote_copy(
-                src_ref=own,
-                dst_ref=landing.at[slot],
-                send_sem=sends.at[base + slot],
-                recv_sem=receives.at[base + slot],
-                device_id=device_at(lax.rem(place + 1 + slot, size)),
-                device_id_type=MESH,
-            )
-            for slot in range(self.count)
-        ]
-
-    def start(self):
-        for copy in self.copies:
-            copy.start()
-
-    def finish(self):
-        total = self.own[...]
-        for slot, copy in enumerate(self.copies):
-            copy.wait_recv()
-            total = total + self.landing[slot]
-        return total
-
-    def drain(self):
-        for copy in self.copies:
-            copy.wait_send()
-
-
-class Shares(Spread):
-    def __init__(self, size, place, device_at, local, landing, sends, receives, base):
-        self.own, self.landing = local.at[place], landing
-        self.count = size - 1
+        send_sem, recv_sem = sends.at[bases[0]], receives.at[bases[1]]
         self.copies = []
-        for slot in range(self.count):
+        for slot in range(size - 1):
             at = lax.rem(place + 1 + slot, size)
             self.copies.append(
                 pltpu.make_async_remote_copy(
-                    src_ref=local.at[at],
+                    src_ref=share_at(at),
                     dst_ref=landing.at[slot],
-                    send_sem=sends.at[base + slot],
-                    recv_sem=receives.at[base + slot],
+                    send_sem=send_sem,
+                    recv_sem=recv_sem,
                     device_id=device_at(at),
                     device_id_type=MESH,
                 )
             )
+        self.all = waiting(landing, send_sem, recv_sem, device_at(lax.rem(place + 1, size)))
+
+    def start(self):
+        for copy in self.copies:
+            copy.start()
+
+    def finish(self):
+        self.all.wait_recv()
+        total = self.own[...]
+        for slot in range(len(self.copies)):
+            total = total + self.landing[slot]
+        return total
+
+    def drain(self):
+        self.all.wait_send()
 
 
 WIDTH = 3584
@@ -194,6 +191,7 @@
     land_cx,
     part_a,
     part_b,
+    part_c,
     part_g,
     part_h,
     land_a1,
@@ -201,6 +199,9 @@
     land_b1,
     land_a2,
     land_b2,
+    land_cross,
+    land_c1,
+    land_c2,
     land_g1,
     land_g2,
     last_src,
@@ -291,26 +292,68 @@
     send_weight = passing(1, weight, weight_other, cross)
     send_grad = passing(2, grad, grad_other, peer)
     send_below = [
-        passing(3 + pair, below.at[pl.ds(128 * pair, 128)], upstream.at[pl.ds(128 * pair, 128)], partner)
-        for pair in range(2)
+        passing(3 + part, below.at[pl.ds(64 * part, 64)], upstream.at[pl.ds(64 * part, 64)], partner)
+        for part in range(4)
     ]
 
-    base = 0
-
-    def spread(size, place, device_at, own, landing):
-        nonlocal base
-        made = Spread(size, place, device_at, own, landing, sends, receives, base)
-        base += made.count
+    bases = (0, 0)
+
+    def spread(size, place, device_at, own, share_at, landing):
+        nonlocal bases
+        made = Spread(size, place, device_at, own, share_at, landing, sends, receives, bases)
+        bases = (bases[0] + 1, bases[1] + 1)
         return made
 
-    count_x = spread(2, x, lambda at: device(z, y, at), counts.at[0], land_cx)
-    count_z = spread(8, z, lambda at: device(at, y, x), counts.at[1], land_cz)
-    count_y = spread(4, y, lambda at: device(z, at, x), counts.at[2], land_cy)
+    def row_spread(size, place, device_at, own, landing):
+        return spread(size, place, device_at, own, lambda at: own, landing)
+
+    count_x = row_spread(2, x, lambda at: device(z, y, at), counts.at[0], land_cx)
+    count_z = row_spread(8, z, lambda at: device(at, y, x), counts.at[1], land_cz)
+    count_y = row_spread(4, y, lambda at: device(z, at, x), counts.at[2], land_cy)
     count_x.start()
 
     @pl.when(pipe == 1)
     def _():
         send_head.start()
+
+    def flow(size, place, ways, local, landing, hops):
+        nonlocal bases
+        made = Flow(size, place, *ways, local, landing, sends, receives, bases, hops)
+        bases = (bases[0] + made.halves, bases[1] + made.count)
+        return made
+
+    z_halves = {(1, 0): 4, (-1, 1): 4, (1, 1): 3, (-1, 0): 3}
+    y_halves = {(1, 0): 2, (-1, 1): 2, (1, 1): 1, (-1, 0): 1}
+    z_whole = {(1, 0): 4, (-1, 0): 3}
+    y_whole = {(1, 0): 2, (-1, 0): 1}
+    rows_of = (pl.ds(0, 64), pl.ds(64, 48))
+    a1 = flow(
+        8,
+        z,
+        z_ways,
+        lambda q, h: part_a.at[q, pl.ds(2 * h, 2), :, pl.ds(0, NEAR - HEAD_DIM)],
+        land_a1,
+        z_halves,
+    )
+    v1 = flow(
+        8,
+        z,
+        z_ways,
+        lambda q, h: part_a.at[q, pl.ds(2 * h, 2), :, pl.ds(NEAR - HEAD_DIM, HEAD_DIM)],
+        land_v1,
+        z_halves,
+    )
+    cx = flow(2, x, (x_way, x_way), lambda q, h: part_c.at[q], land_cross, {(1, 0): 1})
+    c1 = flow(8, z, z_ways, lambda q, h: part_c.at[x, q], land_c1, {(1, 0): 4, (-1, 0): 3})
+    c2 = flow(4, y, y_ways, lambda q, h: part_c.at[x, z, q], land_c2, {(1, 0): 2, (-1, 0): 1})
+    b1 = flow(4, y, y_ways, lambda q, h: part_b.at[pl.ds(4 * h, 4), q], land_b1, y_halves)
+    a2 = flow(4, y, y_ways, lambda q, h: part_a.at[z, q, rows_of[h]], land_a2, y_halves)
+    b2 = flow(8, z, z_ways, lambda q, h: part_b.at[q, y, rows_of[h]], land_b2, z_halves)
+
+    g1 = spread(
+        8, z, lambda at: device(at, y, x), part_g.at[z], lambda at: part_g.at[at], land_g1
+    )
+    g2 = spread(4, y, lambda at: device(z, at, x), part_h.at[y], lambda at: part_h.at[at], land_g2)
 
     loads["inputs"].wait()
 
@@ -385,44 +428,6 @@
         for send in send_below:
             send.wait_recv()
 
-    def flow(size, place, ways, local, landing, hops):
-        nonlocal base
-        first = base
-        made = Flow(
-            size, place, *ways, local, lambda slot: landing.at[slot - first], sends, receives, base, hops
-        )
-        base += made.count
-        return made
-
-    z_halves = {(1, 0): 4, (-1, 1): 4, (1, 1): 3, (-1, 0): 3}
-    y_halves = {(1, 0): 2, (-1, 1): 2, (1, 1): 1, (-1, 0): 1}
-    z_whole = {(1, 0): 4, (-1, 0): 3}
-    y_whole = {(1, 0): 2, (-1, 0): 1}
-    rows_of = (pl.ds(0, 64), pl.ds(64, 48))
-    a1 = flow(
-        8, z, z_ways, lambda q, h: part_a.at[q, pl.ds(2 * h, 2), :, pl.ds(0, SPLIT)], land_a1, z_halves
-    )
-    v1 = flow(
-        8,
-        z,
-        z_ways,
-        lambda q, h: part_a.at[q, pl.ds(2 * h, 2), :, pl.ds(SPLIT, HEAD_DIM)],
-        land_v1,
-        z_halves,
-    )
-    b1 = flow(4, y, y_ways, lambda q, h: part_b.at[pl.ds(4 * h, 4), q], land_b1, y_halves)
-    a2 = flow(4, y, y_ways, lambda q, h: part_a.at[z, q, rows_of[h]], land_a2, y_halves)
-    b2 = flow(8, z, z_ways, lambda q, h: part_b.at[q, y, rows_of[h]], land_b2, z_halves)
-
-    def shares(size, place, device_at, local, landing):
-        nonlocal base
-        made = Shares(size, place, device_at, local, landing, sends, receives, base)
-        base += made.count
-        return made
-
-    g1 = shares(8, z, lambda at: device(at, y, x), part_g, land_g1)
-    g2 = shares(4, y, lambda at: device(z, at, x), part_h, land_g2)
-
     def later_products(index, carry):
         at = pl.ds(pl.multiple_of(index * 896, 128), 896)
         places = pl.ds(2 * index, 2)
@@ -436,19 +441,28 @@
         at = pl.ds(pl.multiple_of(index * 896, 128), 896)
         places = pl.ds(2 * index, 2)
         block = jnp.dot(upstream_turned[at, :], mixed[:, :SPLIT], preferred_element_type=F32)
-        part_a[places, :, :, :SPLIT] = block.astype(BF).reshape(2, 4, 112, SPLIT)
+        crossing = block[:, :CROSS].reshape(2, 4, 2, 56, CROSS).astype(BF)
+        for half in range(2):
+            part_c[half, places] = crossing[:, :, half]
+        part_a[places, :, :, : NEAR - HEAD_DIM] = (
+            block[:, CROSS:].astype(BF).reshape(2, 4, 112, NEAR - HEAD_DIM)
+        )
         return carry
 
     def value_products(index, carry):
         at = pl.ds(pl.multiple_of(index * 896, 128), 896)
         places = pl.ds(2 * index, 2)
         block = jnp.dot(normed[:, at].T, grad[...], preferred_element_type=F32)
-        part_a[places, :, :, SPLIT:] = block.astype(BF).reshape(2, 4, 112, HEAD_DIM)
+        part_a[places, :, :, NEAR - HEAD_DIM :] = block.astype(BF).reshape(2, 4, 112, HEAD_DIM)
         return carry
 
     lax.fori_loop(0, 4, later_products, 0)
     b1.step(0)
     lax.fori_loop(0, 4, first_products, 0)
+    @pl.when(pipe == 0)
+    def _():
+        cx.step(0)
+
     a1.step(0)
 
     def heads_back(first, count):
@@ -480,14 +494,13 @@
     lax.fori_loop(0, 4, unmix, 0)
     send_grad.start()
 
+    @pl.when(pipe == 1)
+    def _():
+        cx.step(0)
+        a1.step(1)
+
     lax.fori_loop(0, 4, value_products, 0)
     v1.step(0)
-    outputs = []
-    for pair in range(2):
-        own_rows = pl.ds(pl.multiple_of((2 * pair + tensor) * LENGTH, LENGTH), LENGTH)
-        outputs.append(
-            pltpu.make_async_copy(below.at[own_rows], cotangent_out.at[pair], load_sems.at[9 + pair])
-        )
 
     def norm_back(index, total):
         at = pl.ds(pl.multiple_of(index * BLOCK, BLOCK), BLOCK)
@@ -512,113 +525,172 @@
             part_g[place // 4, place % 4, :, :112] = gain_row[:, 112 * place : 112 * (place + 1)]
         g1.start()
 
-    def below_pass(pair):
-        rows = pl.ds(128 * pair, 128)
+    def below_pass(part):
+        rows = pl.ds(LENGTH * part, LENGTH)
 
         def through(index, carry):
-            at = pl.ds(pl.multiple_of(index * BLOCK, BLOCK), BLOCK)
+            at = pl.ds(pl.multiple_of(index * 512, 512), 512)
             scaled = normed_grad[rows, at] * gain[:, at]
-            slope = wide(slopes[rows, :])
-            change = wide(rms[rows, :]) * scaled - inputs[rows, at].astype(F32) * slope
+            slope = wide(wide(slopes[rows, :]))
+            change = wide(wide(rms[rows, :])) * scaled - inputs[rows, at].astype(F32) * slope
             below[rows, at] = (upstream[rows, at].astype(F32) + change).astype(BF)
             return carry
 
-        lax.fori_loop(0, BLOCKS, through, 0)
-
-    b1.step(1)
-    a1.step(1)
-
-    @pl.when(pipe == 1)
-    def _():
-        send_weight.wait_recv()
-        pl.semaphore_signal(go, inc=1, device_id=partner, device_id_type=MESH)
-        norm_pass()
+        lax.fori_loop(0, WIDTH // 512, through, 0)
+
+    def write_below(passed=None):
+        for part in range(4):
+            below_pass(part)
+            if passed:
+                passed[part].start()
+        copies = []
         for pair in range(2):
-            below_pass(pair)
-            send_below[pair].start()
-            outputs[pair].start()
-
-    v1.step(1)
-
-    @pl.when(pipe == 0)
-    def _():
-        send_weight.wait_recv()
-        norm_pass()
-
-    a1.step(2)
-    b1.finish()
-    b2.step(0)
-    v1.step(2)
-    a1.step(3)
-    b2.step(1)
-    v1.step(3)
-
-    @pl.when(pipe == 0)
-    def _():
-        for pair in range(2):
-            below_pass(pair)
-            outputs[pair].start()
-
-    b2.step(2)
-    a1.finish()
-    v1.finish()
-    a2.step(0)
-    part_h[...] = g1.finish()
-    g2.start()
-    b2.step(3)
-    a2.step(1)
-    b2.finish()
+            own_rows = pl.ds(pl.multiple_of((2 * pair + tensor) * LENGTH, LENGTH), LENGTH)
+            copy = pltpu.make_async_copy(
+                below.at[own_rows], cotangent_out.at[pair], load_sems.at[9 + pair]
+            )
+            copy.start()
+            copies.append(copy)
+        return copies
 
     def last(index, source, target):
         return pltpu.make_async_remote_copy(
             src_ref=source,
             dst_ref=target,
-            send_sem=sends.at[base + index],
-            recv_sem=receives.at[base + index],
+            send_sem=sends.at[bases[0] + index],
+            recv_sem=receives.at[bases[1] + index],
             device_id=x_way,
             device_id_type=MESH,
         )
 
-    finals = []
-
-    def exchange(index, part):
+    def keep(index, source, target):
+        copy = pltpu.make_async_copy(source, target, load_sems.at[11 + index])
+        copy.start()
+        return copy
+
+    def exchange(index, part, first):
         total = part[z, y].astype(F32)
+        width = total.shape[1]
+        at = pl.ds(first, width)
         low, high = total[:56], total[56:]
-        last_src[index] = jnp.where(x == 0, high, low).astype(BF)
-        copy = last(index, last_src.at[index], landed_out.at[index])
+        last_src[:, at] = jnp.where(x == 0, high, low).astype(BF)
+        copy = last(index, last_src.at[:, at], landed_out.at[:, at])
         copy.start()
-        finals.append(copy)
-        kept[index] = jnp.where(x == 0, low, high)
-        keep = pltpu.make_async_copy(kept.at[index], kept_out.at[index], load_sems.at[11 + index])
-        keep.start()
-        outputs.append(keep)
-
-    exchange(1, part_b)
-    gain_total = g2.finish()
-    low, high = gain_total[:, :56], gain_total[:, 56:112]
-    gain_last[:, :56] = jnp.where(x == 0, high, low)
-    gain_copy = last(2, gain_last, gain_landed_out)
-    gain_copy.start()
-    finals.append(gain_copy)
-    gain_kept[:, :56] = jnp.where(x == 0, low, high)
-    gain_keep = pltpu.make_async_copy(gain_kept, gain_kept_out, load_sems.at[13])
-    gain_keep.start()
-    outputs.append(gain_keep)
-    a2.finish()
-    exchange(0, part_a)
-    for copy in finals:
-        copy.wait_recv()
-    for made in (count_z, count_y, count_x, a1, v1, b1, a2, b2, g1, g2):
-        made.drain()
-    for copy in (*finals, send_weight, send_grad):
-        copy.wait_send()
-    for output in outputs:
-        output.wait()
+        kept[:, at] = jnp.where(x == 0, low, high)
+        return copy, keep(index, kept.at[:, at], kept_out.at[:, at])
+
+    def keep_cross():
+        at = pl.ds(NEAR + COLS, CROSS)
+        kept[:, at] = part_c[x, z, y].astype(F32)
+        return keep(2, kept.at[:, at], kept_out.at[:, at])
+
+    def gain_middle():
+        part_h[...] = g1.finish()
+        g2.start()
+
+    def gain_exchange():
+        total = g2.finish()
+        low, high = total[:, :56], total[:, 56:112]
+        gain_last[:, :56] = jnp.where(x == 0, high, low)
+        copy = last(2, gain_last, gain_landed_out)
+        copy.start()
+        gain_kept[:, :56] = jnp.where(x == 0, low, high)
+        return copy, keep(3, gain_kept, gain_kept_out)
+
+    def settle(finals, locals_):
+        for copy in finals:
+            copy.wait_recv()
+        for made in (cx, a1, v1, b1, c1, a2, b2, c2, g1, g2):
+            made.drain()
+        for copy in finals:
+            copy.wait_send()
+        for copy in locals_:
+            copy.wait()
 
     @pl.when(pipe == 1)
     def _():
+        b1.step(1)
+        send_weight.wait_recv()
+        pl.semaphore_signal(go, inc=1, device_id=partner, device_id_type=MESH)
+        norm_pass()
+        a1.step(2)
+        v1.step(1)
+        copies = write_below(send_below)
+        cx.finish()
+        c1.step(0)
+        a1.step(3)
+        v1.step(2)
+        b1.finish()
+        b2.step(0)
+        c1.step(1)
+        a1.finish()
+        v1.step(3)
+        b2.step(1)
+        c1.step(2)
+        v1.finish()
+        a2.step(0)
+        b2.step(2)
+        c1.step(3)
+        gain_middle()
+        a2.step(1)
+        b2.step(3)
+        c1.finish()
+        c2.step(0)
+        a2.finish()
+        final_a, keep_a = exchange(0, part_a, 0)
+        b2.finish()
+        final_b, keep_b = exchange(1, part_b, NEAR)
+        c2.step(1)
+        final_g, keep_g = gain_exchange()
+        c2.finish()
+        keep_c = keep_cross()
+        settle((final_a, final_b, final_g), (*copies, keep_a, keep_b, keep_g, keep_c))
         for send in send_below:
             send.wait_send()
+
+    @pl.when(pipe == 0)
+    def _():
+        a1.step(1)
+        b1.step(1)
+        cx.finish()
+        c1.step(0)
+        v1.step(1)
+        send_weight.wait_recv()
+        norm_pass()
+        a1.step(2)
+        c1.step(1)
+        v1.step(2)
+        b1.finish()
+        b2.step(0)
+        a1.step(3)
+        c1.step(2)
+        v1.step(3)
+        b2.step(1)
+        a1.finish()
+        c1.step(3)
+        b2.step(2)
+        v1.finish()
+        a2.step(0)
+        c1.finish()
+        c2.step(0)
+        gain_middle()
+        b2.step(3)
+        a2.step(1)
+        c2.step(1)
+        copies = write_below()
+        b2.finish()
+        final_b, keep_b = exchange(1, part_b, NEAR)
+        a2.finish()
+        final_a, keep_a = exchange(0, part_a, 0)
+        final_g, keep_g = gain_exchange()
+        c2.finish()
+        keep_c = keep_cross()
+        settle((final_a, final_b, final_g), (*copies, keep_a, keep_b, keep_g, keep_c))
+
+    for made in (count_z, count_y, count_x):
+        made.drain()
+    for copy in (send_weight, send_grad):
+        copy.wait_send()
 
 
 def last_kernel(
@@ -664,10 +736,11 @@
         load.start()
     for load in loads[:4]:
         load.wait()
-    total = kept[0] + landed[0].astype(F32)
-    mixed[:, :SPLIT] = total[:, :SPLIT]
-    value[...] = total[:, SPLIT:]
-    mixed[:, SPLIT:] = kept[1] + landed[1].astype(F32)
+    total = kept[:, : NEAR + COLS] + landed[...].astype(F32)
+    mixed[:, :CROSS] = kept[:, NEAR + COLS :]
+    mixed[:, CROSS:SPLIT] = total[:, : NEAR - HEAD_DIM]
+    value[...] = total[:, NEAR - HEAD_DIM : NEAR]
+    mixed[:, SPLIT:] = total[:, NEAR:]
     gain[...] = gain_kept[:, :56] + gain_landed[:, :56]
     for store in stores[:3]:
         store.start()
@@ -708,13 +781,13 @@
     reference_logprob,
     sequence_bounds,
 ):
-    copies = 7 + 3 + 1 + 14 + 14 + 6 + 6 + 14 + 7 + 3 + 3
+    send_count, receive_count = 3 + 2 + 5 * 2 + 3 + 3, 3 + 2 + 14 + 14 + 6 + 6 + 14 + 1 + 7 + 3 + 3
     hbm = pl.BlockSpec(memory_space=pl.ANY)
     results = pl.pallas_call(
         step_kernel,
         out_shape=(
-            jax.ShapeDtypeStruct((2, 56, COLS), F32),
-            jax.ShapeDtypeStruct((2, 56, COLS), BF),
+            jax.ShapeDtypeStruct((56, NEAR + COLS + CROSS), F32),
+            jax.ShapeDtypeStruct((56, NEAR + COLS), BF),
             jax.ShapeDtypeStruct((1, 128), F32),
             jax.ShapeDtypeStruct((1, 128), F32),
             jax.ShapeDtypeStruct((2, LENGTH, WIDTH), BF),
@@ -750,27 +823,31 @@
             pltpu.VMEM((7, 1, 128), F32),
             pltpu.VMEM((3, 1, 128), F32),
             pltpu.VMEM((1, 1, 128), F32),
+            pltpu.VMEM((8, 4, 112, NEAR), BF),
             pltpu.VMEM((8, 4, 112, COLS), BF),
-            pltpu.VMEM((8, 4, 112, COLS), BF),
+            pltpu.VMEM((2, 8, 4, 56, CROSS), BF),
             pltpu.VMEM((8, 4, 1, 128), F32),
             pltpu.VMEM((4, 1, 128), F32),
-            pltpu.VMEM((14, 2, 112, SPLIT), BF),
+            pltpu.VMEM((14, 2, 112, NEAR - HEAD_DIM), BF),
             pltpu.VMEM((14, 2, 112, HEAD_DIM), BF),
             pltpu.VMEM((6, 4, 112, COLS), BF),
-            pltpu.VMEM((6, 64, COLS), BF),
+            pltpu.VMEM((6, 64, NEAR), BF),
             pltpu.VMEM((14, 64, COLS), BF),
+            pltpu.VMEM((1, 8, 4, 56, CROSS), BF),
+            pltpu.VMEM((7, 4, 56, CROSS), BF),
+            pltpu.VMEM((3, 56, CROSS), BF),
             pltpu.VMEM((7, 4, 1, 128), F32),
             pltpu.VMEM((3, 1, 128), F32),
-            pltpu.VMEM((2, 56, COLS), BF),
-            pltpu.VMEM((2, 56, COLS), F32),
+            pltpu.VMEM((56, NEAR + COLS), BF),
+            pltpu.VMEM((56, NEAR + COLS + CROSS), F32),
             pltpu.VMEM((1, 128), F32),
             pltpu.VMEM((1, 128), F32),
-            pltpu.SemaphoreType.DMA((14,)),
-            pltpu.SemaphoreType.DMA((5,)),
-            pltpu.SemaphoreType.DMA((5,)),
+            pltpu.SemaphoreType.DMA((15,)),
+            pltpu.SemaphoreType.DMA((7,)),
+            pltpu.SemaphoreType.DMA((7,)),
             pltpu.SemaphoreType.REGULAR,
-            pltpu.SemaphoreType.DMA((copies,)),
-            pltpu.SemaphoreType.DMA((copies,)),
+            pltpu.SemaphoreType.DMA((send_count,)),
+            pltpu.SemaphoreType.DMA((receive_count,)),
         ],
         compiler_params=pltpu.CompilerParams(
             collective_id=0, has_side_effects=True, vmem_limit_bytes=60_000_000

time: 86 us -> 82.3 us (0.957)
  Pallas kernels: 85.3 us -> 81.6 us
    pallas_call x1, Pallas kernels: 82.9 us -> 79.2 us  [body(): pl.pallas_call(step_kernel, out_shape=(jax.ShapeDtypeStruct((56, NEAR + C...]
where the time goes in v5:
time: 82.3 us; the launch traced here: 82.2 us
  Pallas kernels  81.6 us (99%)
    pallas_call x1, Pallas kernels, body(): pl.pallas_call(step_kernel, out_shape=(jax.ShapeDtypeStruct((56, NEAR + C...  79.2 us
    pallas_call x1, Pallas kernels, written_out(): pl.pallas_call(last_kernel, out_shape=shapes, in_specs=[hbm] * 5, out_spe...  2.37 us

profile of v5, /device:TPU:2, one launch (start us, length us, event | category | flops | bytes accessed | tf_op | source)
XLA Modules:
  0.0 82.2 jit_solution(627917856189087782)
XLA Ops:
  0.6 79.2 %shard_map.120 = (f32[56,1024]{1,0:T(8,128)}, bf16[56,896]{1,0:T(8,128)(2,1)}, f32[1,128]{1,0:T(1,128)}, f32[1,128]{1,0:T(1,128)}, bf16[2,64,3584]{2,1,0:T(8,128)(2,1)}) custom-call(s32[2,3]{1,0:T(2,128)} %bounds_hbm.1, f32[2,2]{1,0:T(2,128)} %reference_hbm.1, f32[2,2,64]{2,1,0:T(2,128)} %logprob_hbm.1, f32[1,3584]{1,0:T(1,128)} %gain_hbm.1, ...), custom_call_target="tpu_custom_call" | custom-call | tf_op jit(solution)/shard_map/pallas_call | solution.py:786
  79.9 2.4 %shard_map.121 = (f32[56,896]{1,0:T(8,128)}, f32[56,128]{1,0:T(8,128)}, f32[1,56]{1,0:T(1,128)}, bf16[2,64,3584]{2,1,0:T(8,128)(2,1)}) custom-call(f32[56,1024]{1,0:T(8,128)} %get-tuple-element.13.kept_hbm, bf16[56,896]{1,0:T(8,128)(2,1)} %get-tuple-element.14.landed_hbm, f32[1,128]{1,0:T(1,128)} %get-tuple-element.15.gain_kept_hbm, ...), custom_call_target="tpu_custom_call" | custom-call | tf_op jit(solution)/shard_map/pallas_call | solution.py:761

commit v6 on v5

--- a/solution.py
+++ b/solution.py
@@ -663,9 +663,10 @@
         b1.finish()
         b2.step(0)
         a1.step(3)
+        copies = write_below()
         c1.step(2)
+        b2.step(1)
         v1.step(3)
-        b2.step(1)
         a1.finish()
         c1.step(3)
         b2.step(2)
@@ -677,7 +678,6 @@
         b2.step(3)
         a2.step(1)
         c2.step(1)
-        copies = write_below()
         b2.finish()
         final_b, keep_b = exchange(1, part_b, NEAR)
         a2.finish()
@@ -714,6 +714,7 @@
     load_sems,
     store_sems,
 ):
+    parts = [(pair, pl.ds(32 * half, 32)) for pair in range(2) for half in range(2)]
     loads = [
         pltpu.make_async_copy(source, buffer, load_sems.at[index])
         for index, (source, buffer) in enumerate(
@@ -722,14 +723,19 @@
                 (landed_hbm, landed),
                 (gain_kept_hbm, gain_kept),
                 (gain_landed_hbm, gain_landed),
-                (cotangent_hbm, cotangent),
+                *((cotangent_hbm.at[part], cotangent.at[part]) for part in parts),
             )
         )
     ]
     stores = [
         pltpu.make_async_copy(buffer, target, store_sems.at[index])
         for index, (buffer, target) in enumerate(
-            ((mixed, mixed_hbm), (value, value_hbm), (gain, gain_hbm), (cotangent, cotangent_out))
+            (
+                *((cotangent.at[part], cotangent_out.at[part]) for part in parts),
+                (mixed, mixed_hbm),
+                (value, value_hbm),
+                (gain, gain_hbm),
+            )
         )
     ]
     for load in loads:
@@ -742,10 +748,11 @@
     value[...] = total[:, NEAR - HEAD_DIM : NEAR]
     mixed[:, SPLIT:] = total[:, NEAR:]
     gain[...] = gain_kept[:, :56] + gain_landed[:, :56]
-    for store in stores[:3]:
+    for store in stores[4:]:
         store.start()
-    loads[4].wait()
-    stores[3].start()
+    for load, store in zip(loads[4:], stores[:4]):
+        load.wait()
+        store.start()
     for store in stores:
         store.wait()
 
@@ -765,7 +772,7 @@
         out_specs=(hbm,) * 4,
         scratch_shapes=[pltpu.VMEM(array.shape, array.dtype) for array in arrays]
         + [pltpu.VMEM(shape.shape, shape.dtype) for shape in shapes[:3]]
-        + [pltpu.SemaphoreType.DMA((5,)), pltpu.SemaphoreType.DMA((4,))],
+        + [pltpu.SemaphoreType.DMA((8,)), pltpu.SemaphoreType.DMA((7,))],
         compiler_params=pltpu.CompilerParams(vmem_limit_bytes=60_000_000),
     )(*arrays)
 

time: 82.3 us -> 82.2 us (level)
  no operation moved by 1% of the time
where the time goes in v6:
time: 82.2 us; the launch traced here: 82.1 us
  Pallas kernels  81.5 us (99%)
    pallas_call x1, Pallas kernels, body(): pl.pallas_call(step_kernel, out_shape=(jax.ShapeDtypeStruct((56, NEAR + C...  79.3 us
    pallas_call x1, Pallas kernels, written_out(): pl.pallas_call(last_kernel, out_shape=shapes, in_specs=[hbm] * 5, out_spe...  2.2 us

profile of v6, /device:TPU:2, one launch (start us, length us, event | category | flops | bytes accessed | tf_op | source)
XLA Modules:
  0.0 82.1 jit_solution(7155004480494526815)
XLA Ops:
  0.6 79.3 %shard_map.120 = (f32[56,1024]{1,0:T(8,128)}, bf16[56,896]{1,0:T(8,128)(2,1)}, f32[1,128]{1,0:T(1,128)}, f32[1,128]{1,0:T(1,128)}, bf16[2,64,3584]{2,1,0:T(8,128)(2,1)}) custom-call(s32[2,3]{1,0:T(2,128)} %bounds_hbm.1, f32[2,2]{1,0:T(2,128)} %reference_hbm.1, f32[2,2,64]{2,1,0:T(2,128)} %logprob_hbm.1, f32[1,3584]{1,0:T(1,128)} %gain_hbm.1, ...), custom_call_target="tpu_custom_call" | custom-call | tf_op jit(solution)/shard_map/pallas_call | solution.py:793
  79.9 2.2 %shard_map.121 = (f32[56,896]{1,0:T(8,128)}, f32[56,128]{1,0:T(8,128)}, f32[1,56]{1,0:T(1,128)}, bf16[2,64,3584]{2,1,0:T(8,128)(2,1)}) custom-call(f32[56,1024]{1,0:T(8,128)} %get-tuple-element.13.kept_hbm, bf16[56,896]{1,0:T(8,128)(2,1)} %get-tuple-element.14.landed_hbm, f32[1,128]{1,0:T(1,128)} %get-tuple-element.15.gain_kept_hbm, ...), custom_call_target="tpu_custom_call" | custom-call | tf_op jit(solution)/shard_map/pallas_call | solution.py:768
